TPU v7x, 8 devices: a whole 2x2x1 slice. The times are simulated.
8 devices in a mesh: dp: 1 (over z), tp: 2 (over y), sp: 4 (over x, core).
Axes of the slice: x: 2, y: 2, z: 1, core: 2. Of those that a mesh axis runs over, the one named last changes fastest.
Arguments:
- layer_in: bfloat16 [128, 4096], P('dp')
- new_pos: int32 [128], P('dp')
- k_cache: bfloat16 [128, 512, 8, 128], P('dp', 'sp', 'tp')
- v_cache: bfloat16 [128, 512, 8, 128], P('dp', 'sp', 'tp')
- attn_gain: bfloat16 [4096], replicated
- w_query: bfloat16 [4096, 4096], P(None, 'tp')
- w_key: bfloat16 [4096, 1024], P(None, 'tp')
- w_value: bfloat16 [4096, 1024], P(None, 'tp')
- w_out: bfloat16 [4096, 4096], P('tp')
- mlp_gain: bfloat16 [4096], replicated
- w_gate: bfloat16 [4096, 14336], P(None, 'tp')
- w_up: bfloat16 [4096, 14336], P(None, 'tp')
- w_down: bfloat16 [14336, 4096], P('tp')
Outputs:
- output 1: bfloat16 [128, 4096], P('dp')
- output 2: bfloat16 [128, 512, 8, 128], P('dp', 'sp', 'tp')
- output 3: bfloat16 [128, 512, 8, 128], P('dp', 'sp', 'tp')
- output 4: bfloat16 [128, 8, 128], P('dp', 'tp')
- output 5: bfloat16 [128, 8, 128], P('dp', 'tp')
All inputs are finite; a program needn't handle non-finite values.
Results may differ from a plain program's by a relative error of at most 0.00493161.
Values sent between devices are 32-bit elements.
A program may use at most 1.25 GiB of HBM per device.

v0:
```python
import jax
import jax.numpy as jnp
from jax import lax
from jax.sharding import PartitionSpec as P

ROPE_THETA = 1000000


def rms_norm(in_vec, gain_vec):
    mean_sq = jnp.mean(jnp.square(in_vec), axis=-1, keepdims=True)
    return in_vec * lax.rsqrt(mean_sq + 1e-5) * gain_vec.astype(jnp.float32)


def apply_rotary(in_vec, positions):
    head_dim = in_vec.shape[-1]
    half_idx = jnp.arange(head_dim // 2, dtype=jnp.float32)
    inv_freq = 1.0 / (ROPE_THETA ** (2.0 * half_idx / head_dim))
    angles = positions.astype(jnp.float32)[:, None] * inv_freq[None, :]
    cos_a = jnp.cos(angles)[:, None, :]
    sin_a = jnp.sin(angles)[:, None, :]
    pair_view = in_vec.reshape(in_vec.shape[:-1] + (head_dim // 2, 2))
    even_part = pair_view[..., 0]
    odd_part = pair_view[..., 1]
    rotated = jnp.stack([even_part * cos_a - odd_part * sin_a, even_part * sin_a + odd_part * cos_a], axis=-1)
    return rotated.reshape(in_vec.shape)


def solution(mesh):
    def local_step(layer_in, new_pos, k_blk, v_blk, attn_gain, w_query, w_key, w_value, w_out, mlp_gain, w_gate, w_up, w_down):
        num_rows = layer_in.shape[0]
        blk_len = k_blk.shape[1]
        kv_loc = k_blk.shape[2]
        head_dim = k_blk.shape[3]
        heads_loc = w_query.shape[1] // head_dim
        group_size = heads_loc // kv_loc
        x_f32 = layer_in.astype(jnp.float32)
        normed = rms_norm(x_f32, attn_gain).astype(jnp.bfloat16)
        q_proj = jnp.dot(normed, w_query, preferred_element_type=jnp.float32).reshape(num_rows, heads_loc, head_dim)
        k_proj = jnp.dot(normed, w_key, preferred_element_type=jnp.float32).reshape(num_rows, kv_loc, head_dim)
        v_new = jnp.dot(normed, w_value, preferred_element_type=jnp.float32).reshape(num_rows, kv_loc, head_dim).astype(jnp.bfloat16)
        q_rot = apply_rotary(q_proj, new_pos).astype(jnp.bfloat16)
        k_rot = apply_rotary(k_proj, new_pos).astype(jnp.bfloat16)
        slot_ids = lax.axis_index('sp') * blk_len + jnp.arange(blk_len)
        is_new = (slot_ids[None, :] == new_pos[:, None])[:, :, None, None]
        k_upd = jnp.where(is_new, k_rot[:, None], k_blk)
        v_upd = jnp.where(is_new, v_new[:, None], v_blk)
        q_grp = q_rot.reshape(num_rows, kv_loc, group_size, head_dim)
        scores = jnp.einsum('bkgd,bskd->bkgs', q_grp, k_upd, preferred_element_type=jnp.float32) * (head_dim ** -0.5)
        is_valid = (slot_ids[None, :] <= new_pos[:, None])[:, None, None, :]
        scores = jnp.where(is_valid, scores, -jnp.inf)
        row_max = lax.pmax(jnp.max(scores, axis=-1, keepdims=True), 'sp')
        prob_vals = jnp.exp(scores - row_max)
        denom_sum = lax.psum(jnp.sum(prob_vals, axis=-1, keepdims=True), 'sp')
        part_vals = jnp.einsum('bkgs,bskd->bkgd', prob_vals.astype(jnp.bfloat16), v_upd, preferred_element_type=jnp.float32)
        weighted = lax.psum(part_vals, 'sp')
        attn_vec = (weighted / denom_sum).reshape(num_rows, heads_loc * head_dim).astype(jnp.bfloat16)
        hidden = x_f32 + lax.psum(jnp.dot(attn_vec, w_out, preferred_element_type=jnp.float32), 'tp')
        normed_mlp = rms_norm(hidden, mlp_gain).astype(jnp.bfloat16)
        gate_pre = jnp.dot(normed_mlp, w_gate, preferred_element_type=jnp.float32)
        up_proj = jnp.dot(normed_mlp, w_up, preferred_element_type=jnp.float32)
        act_bf = (jax.nn.silu(gate_pre) * up_proj).astype(jnp.bfloat16)
        mlp_part = jnp.dot(act_bf, w_down, preferred_element_type=jnp.float32)
        layer_out = (hidden + lax.psum(mlp_part, 'tp')).astype(jnp.bfloat16)
        return layer_out, k_upd, v_upd, k_rot, v_new

    cache_spec = P('dp', 'sp', 'tp', None)
    new_spec = P('dp', 'tp', None)
    in_specs = (P('dp', None), P('dp'), cache_spec, cache_spec, P(None), P(None, 'tp'), P(None, 'tp'), P(None, 'tp'), P('tp', None), P(None), P(None, 'tp'), P(None, 'tp'), P('tp', None))
    out_specs = (P('dp', None), cache_spec, cache_spec, new_spec, new_spec)
    return jax.shard_map(local_step, mesh=mesh, in_specs=in_specs, out_specs=out_specs, check_vma=False)
```

profile of v0, /device:TPU:0, one launch (start us, length us, event | category | flops | bytes accessed | tf_op | source)
XLA Modules:
  0.0 342.0 jit_solution(16154626722251451610)
XLA Ops:
  7.3 0.7 convert_element_type.60
  8.0 1.5 fusion.11
  9.5 0.7 convert_element_type.58
  10.2 1.4 broadcast_compare_fusion.1
  11.6 3.3 convolution_convert_fusion
  14.8 0.7 convert_element_type.65
  15.5 4.0 %fusion.27 = f32[128,512]{0,1:T(8,128)S(1)} fusion(bf16[4096,512]{1,0:T(8,128)(2,1)} %param.19, bf16[128,4096]{1,0:T(8,128)(2,1)S(1)} %copy-done, f32[4096]{0:T(1024)S(1)} %convert_element_type.58, f32[128]{0:T(128)S(1)} %add_rsqrt_fusion.1), kind=kOutput, calls=%fused_computation.47 | convolution fusion | flops 538968064 | bytes 5521920 | tf_op jit(solution)/shard_map/dot_general | solution.py:39
  19.7 0.3 subtract_convert_fusion.1
  20.1 0.3 pad_maximum_fusion.1
  20.3 0.8 copy.22
  21.1 10.2 %fusion.29 = f32[128,2048]{0,1:T(8,128)S(1)} fusion(bf16[4096,2048]{1,0:T(8,128)(2,1)} %param.18, bf16[128,4096]{1,0:T(8,128)(2,1)S(1)} %copy-done, f32[4096]{0:T(1024)S(1)} %convert_element_type.58, f32[128]{0:T(128)S(1)} %add_rsqrt_fusion.1), kind=kOutput, calls=%fused_computation.48 | convolution fusion | flops 2149580800 | bytes 18891264 | tf_op jit(solution)/shard_map/dot_general | solution.py:38
  31.4 1.4 subtract_convert_fusion
  32.7 1.2 pad_maximum_fusion
  33.9 1.2 copy.23
  35.1 29.1 %broadcast_select_fusion.1 = (bf16[128,128,4,128]{3,2,1,0:T(4,128)(2,1)S(1)}, bf16[128,128,4,128]{3,2,1,0:T(4,128)(2,1)}) fusion(bf16[128,128,4,128]{3,2,1,0:T(4,128)(2,1)} %param.15, pred[128,128]{1,0:T(8,128)(4,1)} %get-tuple-element.17, bf16[128,4,128]{2,1,0:T(4,128)(2,1)} %copy.22, bf16[128,128,4,128]{3,2,1,0:T(4,128)(2,1)} %param.16, ...), kind=kLoop, calls=%fused_computation.5 | loop fusion | flops 16777216 | bytes 67387392 | tf_op jit(solution)/shard_map/jit(_where)/select_n | solution.py:45
  64.2 12.0 %fusion.31 = (f32[128,4,4]{2,1,0:T(4,128)}, f32[128,4,4,128]{3,2,1,0:T(4,128)}) fusion(bf16[128,4,4,128]{3,2,1,0:T(4,128)(2,1)} %copy.23, bf16[128,128,4,128]{3,2,1,0:T(4,128)(2,1)S(1)} %get-tuple-element.14, pred[128,128]{1,0:T(8,128)(4,1)} %get-tuple-element.16), kind=kOutput, calls=%fused_computation.49 | convolution fusion | flops 67893248 | bytes 18374656 | tf_op jit(solution)/shard_map/bkgd,bskd->bkgs/dot_general | solution.py:48
  76.1 17.3 %pmax.7 = f32[128,4,4]{2,1,0:T(4,128)S(1)} all-reduce(f32[128,4,4]{2,1,0:T(4,128)} %get-tuple-element.20), channel_id=1, replica_groups=mesh['dp'=1,'tp'=2,'sp'=4] {'sp'}, use_global_device_ids=true, to_apply=%region_2.3 | all-reduce | flops 2048 | bytes 16384 | tf_op jit(solution)/shard_map/pmax | solution.py:51
  93.5 12.4 %fusion = f32[128,4,4,128]{3,2,1,0:T(4,128)} fusion(bf16[128,128,4,128]{3,2,1,0:T(4,128)(2,1)} %get-tuple-element.15, f32[128,4,4,128]{3,2,1,0:T(4,128)} %get-tuple-element.21, f32[128,4,4]{2,1,0:T(4,128)S(1)} %pmax.7), kind=kOutput, calls=%fused_computation | convolution fusion | flops 67633152 | bytes 18882560 | tf_op jit(solution)/shard_map/bkgs,bskd->bkgd/dot_general | solution.py:54
  105.9 1.4 fusion.21
  107.3 17.6 %psum.29 = f32[128,4,4]{2,1,0:T(4,128)S(1)} all-reduce(f32[128,4,4]{2,1,0:T(4,128)S(1)} %fusion.21), channel_id=1, replica_groups=mesh['dp'=1,'tp'=2,'sp'=4] {'sp'}, use_global_device_ids=true, to_apply=%region_5.6 | all-reduce | flops 2048 | bytes 16384 | tf_op jit(solution)/shard_map/psum | solution.py:53
  124.9 14.5 %all-reduce.4.cloned.1.call-done = f32[128,4,4,128]{3,2,1,0:T(4,128)} async-done(((f32[128,4,4,128]{3,2,1,0:T(4,128)}), f32[128,4,4,128]{3,2,1,0:T(4,128)}) %all-reduce.4.cloned.1.call-update) | async-done | bytes 1048592 | tf_op jit(solution)/shard_map/psum | solution.py:55
  139.4 1.8 divide_convert_fusion
  141.1 0.4 convert_element_type.67
  141.6 9.4 %fusion.32 = f32[128,4096]{1,0:T(8,128)} fusion(bf16[128,2048]{1,0:T(8,128)(2,1)S(1)} %convert_element_type.67, bf16[2048,4096]{1,0:T(8,128)(2,1)} %param.21), kind=kOutput, calls=%fused_computation.50 | convolution fusion | flops 2147483648 | bytes 19398656 | tf_op jit(solution)/shard_map/dot_general | solution.py:57
  151.1 57.5 %all-reduce.6.cloned.1.call-done = f32[128,4096]{1,0:T(8,128)} async-done(((f32[128,4096]{1,0:T(8,128)}), f32[128,4096]{1,0:T(8,128)}) %all-reduce.6.cloned.1.call-update) | async-done | bytes 2097168 | tf_op jit(solution)/shard_map/psum | solution.py:57
  208.5 2.1 multiply_reduce_fusion
  210.7 0.4 multiply_convert_fusion
  211.1 1.0 copy-done.3
  212.1 21.9 %fusion.33 = f32[128,7168]{1,0:T(8,128)} fusion(bf16[128,4096]{1,0:T(8,128)(2,1)S(1)} %multiply_convert_fusion, bf16[4096,7168]{1,0:T(8,128)(2,1)} %param.23), kind=kOutput, calls=%fused_computation.51 | convolution fusion | flops 7516192768 | bytes 63438848 | tf_op jit(solution)/shard_map/dot_general | solution.py:59
  234.0 41.3 %fusion.5 = f32[128,4096]{1,0:T(8,128)} fusion(bf16[7168,4096]{1,0:T(8,128)(2,1)} %param.25, bf16[128,4096]{1,0:T(8,128)(2,1)} %copy-done.3, bf16[4096,7168]{1,0:T(8,128)(2,1)} %param.24, f32[128,7168]{1,0:T(8,128)} %fusion.33), kind=kOutput, calls=%fused_computation.8 | convolution fusion | flops 15037890560 | bytes 124256256 | tf_op jit(solution)/shard_map/dot_general | solution.py:62
  275.3 57.3 %all-reduce.8.cloned.1.call-done = f32[128,4096]{1,0:T(8,128)} async-done(((f32[128,4096]{1,0:T(8,128)}), f32[128,4096]{1,0:T(8,128)}) %all-reduce.8.cloned.1.call-update) | async-done | bytes 2097168 | tf_op jit(solution)/shard_map/psum | solution.py:63
  332.6 2.9 add_convert_fusion
  (23 shorter events, 0.5 us)
Async XLA Ops:
  7.2 8.4 %copy-start = (bf16[128,4096]{1,0:T(8,128)(2,1)S(1)}, bf16[128,4096]{1,0:T(8,128)(2,1)}, u32[]{:S(2)}) copy-start(bf16[128,4096]{1,0:T(8,128)(2,1)} %param.13) | copy-start | bytes 3145732
  7.2 132.2 %all-reduce.4.cloned.1.call-start = ((), (), s32[]{:S(2)}) async-start(), calls=%async_computation | async-start | bytes 2097152 | tf_op jit(solution)/shard_map/psum | solution.py:55
  64.2 12.0 %copy-start.2 = (bf16[128,128,4,128]{3,2,1,0:T(4,128)(2,1)}, bf16[128,128,4,128]{3,2,1,0:T(4,128)(2,1)S(1)}, u32[]{:S(2)}) copy-start(bf16[128,128,4,128]{3,2,1,0:T(4,128)(2,1)S(1)} %get-tuple-element.14) | copy-start | bytes 50331652
  93.4 12.5 %copy-start.4 = (f32[128,4,4,128]{3,2,1,0:T(4,128)S(1)}, f32[128,4,4,128]{3,2,1,0:T(4,128)}, u32[]{:S(2)}) copy-start(f32[128,4,4,128]{3,2,1,0:T(4,128)} %get-tuple-element.21) | copy-start | bytes 3145732
  105.9 102.6 %all-reduce.6.cloned.1.call-start = ((), (), s32[]{:S(2)}) async-start(), calls=%async_computation.1 | async-start | bytes 4194304 | tf_op jit(solution)/shard_map/psum | solution.py:57
  141.5 9.5 %copy-start.5 = (bf16[4096]{0:T(1024)(128)(2,1)S(1)}, bf16[4096]{0:T(1024)(128)(2,1)}, u32[]{:S(2)}) copy-start(bf16[4096]{0:T(1024)(128)(2,1)} %param.22) | copy-start | bytes 24580
  151.0 181.6 %all-reduce.8.cloned.1.call-start = ((), (), s32[]{:S(2)}) async-start(), calls=%async_computation.2 | async-start | bytes 4194304 | tf_op jit(solution)/shard_map/psum | solution.py:63
  208.5 2.2 copy-start.1
  211.1 1.0 copy-start.3
Sparse Core Ops, SparseCore 0:
  106.0 33.3 all-reduce.3
  151.1 57.3 all-reduce.5
  275.4 57.0 all-reduce.7
where the time goes:
time: 342 us
  waiting for transfers between devices  129 us (38%)
  matrix products  114 us (33%)
  other arithmetic  45.2 us (13%)
  blocking collectives  34.9 us (10%)
  between operations  13.9 us (4%)
  local copies, waits for them, and re-layouts  4.17 us (1%)
    psum x1, waiting for transfers between devices, local_step(): lax.psum(jnp.dot(attn_vec, w_out, preferred_element_type=jnp.float32), 'tp')  57.5 us
    psum x1, waiting for transfers between devices, local_step(): layer_out = (hidden + lax.psum(mlp_part, 'tp')).astype(jnp.bfloat16)  57.3 us
    dot_general x1, matrix products, local_step(): mlp_part = jnp.dot(act_bf, w_down, preferred_element_type=jnp.float32)  41.3 us
    select_n x1, other arithmetic, local_step(): k_upd = jnp.where(is_new, k_rot[:, None], k_blk)  29.1 us
    dot_general x1, matrix products, local_step(): gate_pre = jnp.dot(normed_mlp, w_gate, preferred_element_type=jnp.float32)  21.9 us
    psum x1, blocking collectives, local_step(): denom_sum = lax.psum(jnp.sum(prob_vals, axis=-1, keepdims=True), 'sp')  17.6 us
    pmax x1, blocking collectives, local_step(): row_max = lax.pmax(jnp.max(scores, axis=-1, keepdims=True), 'sp')  17.3 us
    psum x1, waiting for transfers between devices, local_step(): weighted = lax.psum(part_vals, 'sp')  14.5 us
  transfers between devices with their start and end apart: 3, of which 3 were waited for; matrix products, arithmetic and copies ran while one was open for 0% of the time, Pallas kernels for 0%

commit v1 on v0

v1 whole, which is shorter than its diff:
```python
import functools

import jax
import jax.numpy as jnp
import numpy as np
from jax import lax
from jax.experimental import pallas as pl
from jax.experimental.pallas import tpu as pltpu
from jax.sharding import PartitionSpec as P

ROPE_THETA = 1000000
MESH = pl.DeviceIdType.MESH
F32 = jnp.float32
BF16 = jnp.bfloat16
MIB = 2**20

ROWS = 128
DIM = 4096
HD = 128
SLOTS = 128
KVH = 4
QH = 16
HID = 7168
HSL = HID // 4
NEG = -1e30

RING = 4
WRING = 3


def rms(x, gain):
    ms = jnp.mean(jnp.square(x), axis=-1, keepdims=True)
    return x * lax.rsqrt(ms + 1e-5) * gain.astype(F32)


def attn_kernel(
    pos_s, x_ref, pos_v, freq_ref, gain_ref, wq, wk, wv, k_in, v_in,
    k_out, v_out, o_out, kn_out, vn_out,
    n_s, wbuf, kbuf, vbuf, qf, kf, vf, kdup, vdup, wsem, isem, osem,
):
    sp = lax.axis_index("sp")
    wsrc = [wk, wv] + [wq.at[:, pl.ds(512 * j, 512)] for j in range(4)]

    def wcopy(j):
        return pltpu.make_async_copy(wsrc[j], wbuf.at[j % WRING], wsem.at[j % WRING])

    def copies_in(i, s):
        rows = pl.ds(i * 16, 16)
        return (
            pltpu.make_async_copy(k_in.at[rows], kbuf.at[s], isem.at[0, s]),
            pltpu.make_async_copy(v_in.at[rows], vbuf.at[s], isem.at[1, s]),
        )

    def copies_out(i, s):
        rows = pl.ds(i * 16, 16)
        return (
            pltpu.make_async_copy(kbuf.at[s], k_out.at[rows], osem.at[0, s]),
            pltpu.make_async_copy(vbuf.at[s], v_out.at[rows], osem.at[1, s]),
        )

    for j in range(WRING):
        wcopy(j).start()
    for i in range(2):
        for c in copies_in(i, i):
            c.start()

    n_s[...] = rms(x_ref[...].astype(F32), gain_ref[...]).astype(BF16)
    ang = pos_v[...].astype(F32) * freq_ref[...]
    lane = lax.broadcasted_iota(jnp.int32, (ROWS, HD), 1)
    even = (lane & 1) == 0
    cosr = jnp.cos(ang)
    sinr = jnp.sin(ang)
    sinr = jnp.where(even, -sinr, sinr)

    def rotate(y):
        swap = jnp.where(even, pltpu.roll(y, HD - 1, 1), pltpu.roll(y, 1, 1))
        return y * cosr + swap * sinr

    for j in range(6):
        wcopy(j).wait()
        y = jnp.dot(n_s[...], wbuf[j % WRING], preferred_element_type=F32)
        if j + WRING < 6:
            wcopy(j + WRING).start()
        for hh in range(4):
            yh = y[:, hh * HD : (hh + 1) * HD]
            if j != 1:
                yh = rotate(yh)
            if j >= 2:
                qf[pl.ds((j - 2) * 4 + hh, ROWS, stride=QH), :] = yh
            else:
                one, dup = (kf, kdup) if j == 0 else (vf, vdup)
                one[pl.ds(hh, ROWS, stride=KVH), :] = yh
                for rep in range(4):
                    dup[pl.ds(rep * KVH + hh, ROWS, stride=16), :] = yh
    kn_out[...] = kf[...].astype(BF16)
    vn_out[...] = vf[...].astype(BF16)

    col = lax.broadcasted_iota(jnp.int32, (QH, SLOTS * KVH), 1)
    hrow = lax.broadcasted_iota(jnp.int32, (QH, SLOTS * KVH), 0)
    head_ok = (col & 3) == (hrow >> 2)
    slot_id = jnp.where(head_ok, col >> 2, jnp.int32(1 << 20))
    r16 = lax.broadcasted_iota(jnp.int32, (16, HD), 0) >> 2
    eye = lax.broadcasted_iota(jnp.int32, (128, 128), 0) == lax.broadcasted_iota(
        jnp.int32, (128, 128), 1
    )

    def block(r, _):
        s = lax.rem(r, RING)
        for c in copies_in(r, s):
            c.wait()

        lims = []
        for b in range(16):
            row = r * 16 + b
            lim = pos_s[row] - sp * SLOTS
            lims.append(lim)
            cl = jnp.clip(lim, 0, SLOTS - 1)
            at = pl.ds(pl.multiple_of((cl >> 2) * 16, 16), 16)
            hit = r16 == jnp.where(lim == cl, cl & 3, -1)
            new = pl.ds(pl.multiple_of(row * 16, 16), 16)
            kbuf[s, b, at, :] = jnp.where(hit, kdup[new, :].astype(BF16), kbuf[s, b, at, :])
            vbuf[s, b, at, :] = jnp.where(hit, vdup[new, :].astype(BF16), vbuf[s, b, at, :])

        for c in copies_out(r, s):
            c.start()

        for half in range(2):
            sc = []
            for b in range(8):
                row = r * 16 + half * 8 + b
                q = qf[pl.ds(pl.multiple_of(row * QH, QH), QH), :].astype(BF16)
                t = lax.dot_general(
                    q, kbuf[s, half * 8 + b], (((1,), (1,)), ((), ())),
                    preferred_element_type=F32,
                )
                sc.append(t)
            ms, ls = [], []
            for b in range(8):
                ok = slot_id <= lims[half * 8 + b]
                t = jnp.where(ok, sc[b] * (HD**-0.5), NEG)
                m = jnp.maximum(jnp.max(t, axis=-1, keepdims=True), NEG * 0.1)
                w = jnp.exp(t - m)
                ms.append(m)
                ls.append(jnp.sum(w, axis=-1, keepdims=True))
                o = jnp.dot(w.astype(BF16), vbuf[s, half * 8 + b], preferred_element_type=F32)
                o_out[r, pl.ds((half * 8 + b) * QH, QH), :] = o
            m = jnp.concatenate(ms, axis=0)
            l = jnp.concatenate(ls, axis=0)
            o_out[r, pl.ds(256 + half, 1), :] = jnp.sum(jnp.where(eye, m, 0.0), axis=0, keepdims=True)
            o_out[r, pl.ds(258 + half, 1), :] = jnp.sum(jnp.where(eye, l, 0.0), axis=0, keepdims=True)

        @pl.when(r + 2 < 8)
        def _():
            s2 = lax.rem(r + 2, RING)

            @pl.when(r >= 2)
            def _():
                for c in copies_out(r - 2, s2):
                    c.wait()

            for c in copies_in(r + 2, s2):
                c.start()

        return 0

    lax.fori_loop(0, 8, block, 0)
    for i in range(4, 8):
        for c in copies_out(i, i % RING):
            c.wait()


def run_attn(pos, x, gain, wq, wk, wv, k_blk, v_blk):
    half_idx = np.arange(HD // 2, dtype=np.float32)
    inv = (1.0 / np.power(np.float32(ROPE_THETA), np.float32(2.0) * half_idx / np.float32(HD))).astype(np.float32)
    freq = jnp.asarray(np.repeat(inv, 2)[None, :])
    vm = pl.BlockSpec(memory_space=pltpu.VMEM)
    hbm = pl.BlockSpec(memory_space=pl.ANY)
    cache = jax.ShapeDtypeStruct((ROWS, SLOTS * KVH, HD), BF16)
    new = jax.ShapeDtypeStruct((ROWS * KVH, HD), BF16)
    return pl.pallas_call(
        attn_kernel,
        name="attn",
        out_shape=[cache, cache, jax.ShapeDtypeStruct((8, 264, 128), F32), new, new],
        in_specs=[pl.BlockSpec(memory_space=pltpu.SMEM), vm, vm, vm, vm] + [hbm] * 5,
        out_specs=[hbm, hbm, vm, vm, vm],
        scratch_shapes=[
            pltpu.VMEM((ROWS, DIM), BF16),
            pltpu.VMEM((WRING, DIM, 512), BF16),
            pltpu.VMEM((RING, 16, SLOTS * KVH, HD), BF16),
            pltpu.VMEM((RING, 16, SLOTS * KVH, HD), BF16),
            pltpu.VMEM((ROWS * QH, HD), F32),
            pltpu.VMEM((ROWS * KVH, HD), F32),
            pltpu.VMEM((ROWS * KVH, HD), F32),
            pltpu.VMEM((ROWS * 16, HD), F32),
            pltpu.VMEM((ROWS * 16, HD), F32),
            pltpu.SemaphoreType.DMA((WRING,)),
            pltpu.SemaphoreType.DMA((2, RING)),
            pltpu.SemaphoreType.DMA((2, RING)),
        ],
        compiler_params=pltpu.CompilerParams(vmem_limit_bytes=56 * MIB),
        cost_estimate=pl.CostEstimate(flops=4 * 10**9, bytes_accessed=92 * 10**6, transcendentals=10**6),
    )(
        pos, x, pos[:, None], freq, gain[None, :], wq, wk, wv,
        k_blk.reshape(ROWS, SLOTS * KVH, HD), v_blk.reshape(ROWS, SLOTS * KVH, HD),
    )


NC = 8
CW = DIM // NC
HC = CW // 2


def tail_kernel(
    o_in, x_in, gain_ref, wo, wg, wu, wd,
    out_ref,
    wo_v, wg_v, wu_v, rb1, ob, rb2, ofin, obf, wp, ry, hs, xs, gat, nbf, act,
    part, rd, r1, r2, gat2, wsem, bsem, ysem, gsem, fsem,
):
    sp = lax.axis_index("sp")
    yi = lax.axis_index("tp")
    dp = lax.axis_index("dp")
    core = lax.rem(sp, 2)
    xi = sp // 2
    dev_c = (dp, yi, sp + 1 - 2 * core)
    dev_x = (dp, yi, lax.rem(sp + 2, 4))
    dev_y = (dp, 1 - yi, sp)
    me = core * 4 + xi * 2 + yi
    me_x = core * 4 + (1 - xi) * 2 + yi
    me_y = core * 4 + xi * 2 + 1 - yi
    me_xy = core * 4 + (1 - xi) * 2 + 1 - yi

    def rc(src, dst, sems, dev):
        return pltpu.make_async_remote_copy(
            src_ref=src, dst_ref=dst, send_sem=sems.at[0], recv_sem=sems.at[1],
            device_id=dev, device_id_type=MESH,
        )

    bar = pltpu.get_barrier_semaphore()
    for dev in (dev_c, dev_x, dev_y):
        pl.semaphore_signal(bar, inc=1, device_id=dev, device_id_type=MESH)
    pl.semaphore_wait(bar, 3)

    b1 = rc(o_in.at[pl.ds(4 * (1 - core), 4)], rb1, bsem.at[0], dev_c)
    b1.start()
    hcols = pl.ds(pl.multiple_of(sp * HSL, 128), HSL)
    hrows = pl.ds(pl.multiple_of(sp * HSL, 128), HSL)
    cx = pltpu.make_async_copy(x_in.at[me], xs, wsem.at[0])
    cwo = pltpu.make_async_copy(wo, wo_v, wsem.at[1])
    cwg = pltpu.make_async_copy(wg.at[:, hcols], wg_v, wsem.at[2])
    cwu = pltpu.make_async_copy(wu.at[:, hcols], wu_v, wsem.at[3])
    cwd = pltpu.make_async_copy(wd.at[hrows], wo_v.at[pl.ds(0, HSL)], wsem.at[4])
    for c in (cx, cwo, cwg, cwu):
        c.start()

    def column(v):
        return jnp.transpose(jnp.broadcast_to(v, (128, 128)))

    def merge(a, b, put, last):
        m1, m2 = a[pl.ds(256, 2), :], b[pl.ds(256, 2), :]
        l1, l2 = a[pl.ds(258, 2), :], b[pl.ds(258, 2), :]
        m = jnp.maximum(m1, m2)
        a1 = jnp.exp(m1 - m)
        a2 = jnp.exp(m2 - m)
        l = a1 * l1 + a2 * l2
        if last:
            a1 = a1 / l
            a2 = a2 / l
        for g in range(2):
            rows = pl.ds(g * 128, 128)
            put(g, column(a1[g : g + 1]) * a[rows, :] + column(a2[g : g + 1]) * b[rows, :])
        return m, l

    b1.wait_recv()

    def first(q):
        dst = ob.at[q]

        def put(g, v):
            dst[pl.ds(g * 128, 128), :] = v

        m, l = merge(o_in.at[4 * core + q], rb1.at[q], put, False)
        dst[pl.ds(256, 2), :] = m
        dst[pl.ds(258, 2), :] = l

    first(2 * (1 - xi))
    first(2 * (1 - xi) + 1)
    b2 = rc(ob.at[pl.ds(2 * (1 - xi), 2)], rb2, bsem.at[1], dev_x)
    b2.start()
    first(2 * xi)
    first(2 * xi + 1)
    b2.wait_recv()
    for q in range(2):

        def put(g, v):
            ofin[pl.ds(q * 256 + g * 128, 128), :] = v

        merge(ob.at[2 * xi + q], rb2.at[q], put, True)
    for h in range(QH):
        obf[:, h * HD : (h + 1) * HD] = ofin[pl.ds(h, 32, stride=QH), :].astype(BF16)

    cwo.wait()
    NY = 4
    YW = DIM // NY
    ycp = []
    for j in range(NY):

        def ostep(i, _):
            cols = pl.ds(pl.multiple_of(j * YW + i * 512, 512), 512)
            v = jnp.dot(obf[...], wo_v[:, cols], preferred_element_type=F32)
            wp[:, :, cols] = v.reshape(2, 16, 512)
            return 0

        lax.fori_loop(0, YW // 512, ostep, 0)
        cols = pl.ds(j * YW, YW)
        c = rc(wp.at[1 - yi, :, cols], ry.at[:, cols], ysem.at[j], dev_y)
        c.start()
        ycp.append(c)
    cwd.start()
    cx.wait()
    for j in range(NY):
        cols = pl.ds(j * YW, YW)
        ycp[j].wait_recv()
        hs[:, cols] = xs[:, cols].astype(F32) + wp[yi, :, cols] + ry[:, cols]
    gat[me] = rms(hs[...], gain_ref[...]).astype(BF16).astype(F32)

    def gather0(buf, c0, w, sems):
        cs = pl.ds(c0, w)
        out = []
        for k, dev in ((0, dev_x), (1, dev_y), (2, dev_c)):
            c = rc(buf.at[me, :, cs], buf.at[me, :, cs], sems.at[k], dev)
            c.start()
            out.append(c)
        return out

    def gather1(buf, c0, w, sems, cps):
        lo, hi, cs = pl.ds(c0, w // 2), pl.ds(c0 + w // 2, w // 2), pl.ds(c0, w)
        cps[0].wait_recv()
        a = rc(buf.at[me_x, :, lo], buf.at[me_x, :, lo], sems.at[3], dev_y)
        a.start()
        b = rc(buf.at[me_x, :, cs], buf.at[me_x, :, cs], sems.at[4], dev_c)
        b.start()
        cps[1].wait_recv()
        c = rc(buf.at[me_y, :, hi], buf.at[me_y, :, hi], sems.at[5], dev_x)
        c.start()
        d = rc(buf.at[me_y, :, cs], buf.at[me_y, :, cs], sems.at[6], dev_c)
        d.start()
        return [a, b, c, d]

    def gather2(buf, c0, w, sems, cps):
        cs = pl.ds(c0, w)
        cps[0].wait_recv()
        cps[2].wait_recv()
        c = rc(buf.at[me_xy, :, cs], buf.at[me_xy, :, cs], sems.at[7], dev_c)
        c.start()
        return [c]

    g0 = gather0(gat, 0, DIM, gsem)
    g1 = gather1(gat, 0, DIM, gsem, g0)
    g2 = gather2(gat, 0, DIM, gsem, g1)
    for c in (g0[2], g1[1], g1[3], g2[0]):
        c.wait_recv()

    def cast(r, _):
        nbf[pl.ds(pl.multiple_of(r * 16, 16), 16), :] = gat[r].astype(BF16)
        return 0

    lax.fori_loop(0, 8, cast, 0)
    cwg.wait()
    cwu.wait()

    def up(i, _):
        cols = pl.ds(pl.multiple_of(i * 256, 256), 256)
        g = jnp.dot(nbf[...], wg_v[:, cols], preferred_element_type=F32)
        u = jnp.dot(nbf[...], wu_v[:, cols], preferred_element_type=F32)
        act[:, cols] = (jax.nn.silu(g) * u).astype(BF16)
        return 0

    lax.fori_loop(0, HSL // 256, up, 0)
    cwd.wait()

    state = [dict() for _ in range(NC)]

    def s0(j):
        cs = pl.ds(j * CW, CW)
        v = jnp.dot(act[...], wo_v[pl.ds(0, HSL), cs], preferred_element_type=F32)
        part[:, :, cs] = v.reshape(8, 16, CW)
        c = rc(part.at[pl.ds(4 * (1 - core), 4), :, cs], rd.at[:, :, cs], fsem.at[j, 8], dev_c)
        c.start()
        state[j]["d"] = c

    def s1(j):
        cs = pl.ds(j * CW, CW)
        state[j]["d"].wait()
        mine = pl.ds(4 * core, 4)
        rd[:, :, cs] = part[mine, :, cs] + rd[:, :, cs]
        if j % 2 == 0:
            c = [rc(rd.at[pl.ds(2 * (1 - xi), 2), :, cs], r1.at[:, :, cs], fsem.at[j, 9], dev_x)]
        else:
            c = [
                rc(rd.at[2 * i + 1 - yi, :, cs], r1.at[i, :, cs], fsem.at[j, 9 + i], dev_y)
                for i in range(2)
            ]
        for k in c:
            k.start()
        state[j]["r"] = c

    def s2(j):
        cs = pl.ds(j * CW, CW)
        for k in state[j]["r"]:
            k.wait_recv()
        if j % 2 == 0:
            for i in range(2):
                r1[i, :, cs] = r1[i, :, cs] + rd[2 * xi + i, :, cs]
            c = rc(r1.at[1 - yi, :, cs], r2.at[:, cs], fsem.at[j, 11], dev_y)
        else:
            for i in range(2):
                r1[i, :, cs] = r1[i, :, cs] + rd[2 * i + yi, :, cs]
            c = rc(r1.at[1 - xi, :, cs], r2.at[:, cs], fsem.at[j, 11], dev_x)
        c.start()
        state[j]["r2"] = c

    def s3(j):
        cs = pl.ds(j * CW, CW)
        state[j]["r2"].wait_recv()
        own = r1[yi, :, cs] if j % 2 == 0 else r1[xi, :, cs]
        y = hs[:, cs] + (own + r2[:, cs])
        gat2[me, :, cs] = y.astype(BF16).astype(F32)
        state[j]["g0"] = gather0(gat2, j * CW, CW, fsem.at[j])

    def s4(j):
        state[j]["g1"] = gather1(gat2, j * CW, CW, fsem.at[j], state[j]["g0"])

    def s5(j):
        state[j]["g2"] = gather2(gat2, j * CW, CW, fsem.at[j], state[j]["g1"])

    def s6(j):
        cs = pl.ds(j * CW, CW)
        st = state[j]
        for c in (st["g0"][2], st["g1"][1], st["g1"][3], st["g2"][0]):
            c.wait_recv()
        out_ref[:, :, cs] = gat2[:, :, cs].astype(BF16)

    stages = (s0, s1, s2, s3, s4, s5, s6)
    for t in range(NC + len(stages) - 1):
        for k, stage in enumerate(stages):
            if 0 <= t - k < NC:
                stage(t - k)

    b1.wait_send()
    b2.wait_send()
    for c in ycp + g0 + g1 + g2:
        c.wait_send()
    for st in state:
        for c in st["r"] + [st["r2"]] + st["g0"] + st["g1"] + st["g2"]:
            c.wait_send()


def run_tail(o_part, x, gain, wo, wg, wu, wd):
    vm = pl.BlockSpec(memory_space=pltpu.VMEM)
    hbm = pl.BlockSpec(memory_space=pl.ANY)
    return pl.pallas_call(
        tail_kernel,
        name="tail",
        out_shape=jax.ShapeDtypeStruct((8, 16, DIM), BF16),
        in_specs=[vm, hbm, vm, hbm, hbm, hbm, hbm],
        out_specs=vm,
        scratch_shapes=[
            pltpu.VMEM((2048, DIM), BF16),
            pltpu.VMEM((DIM, HSL), BF16),
            pltpu.VMEM((DIM, HSL), BF16),
            pltpu.VMEM((4, 264, 128), F32),
            pltpu.VMEM((4, 264, 128), F32),
            pltpu.VMEM((2, 264, 128), F32),
            pltpu.VMEM((512, 128), F32),
            pltpu.VMEM((32, 2048), BF16),
            pltpu.VMEM((2, 16, DIM), F32),
            pltpu.VMEM((16, DIM), F32),
            pltpu.VMEM((16, DIM), F32),
            pltpu.VMEM((16, DIM), BF16),
            pltpu.VMEM((8, 16, DIM), F32),
            pltpu.VMEM((ROWS, DIM), BF16),
            pltpu.VMEM((ROWS, HSL), BF16),
            pltpu.VMEM((8, 16, DIM), F32),
            pltpu.VMEM((4, 16, DIM), F32),
            pltpu.VMEM((2, 16, DIM), F32),
            pltpu.VMEM((16, DIM), F32),
            pltpu.VMEM((8, 16, DIM), F32),
            pltpu.SemaphoreType.DMA((5,)),
            pltpu.SemaphoreType.DMA((2, 2)),
            pltpu.SemaphoreType.DMA((4, 2)),
            pltpu.SemaphoreType.DMA((8, 2)),
            pltpu.SemaphoreType.DMA((NC, 12, 2)),
        ],
        compiler_params=pltpu.CompilerParams(
            collective_id=0, has_side_effects=True, vmem_limit_bytes=67043328
        ),
        cost_estimate=pl.CostEstimate(flops=6 * 10**9, bytes_accessed=62 * 10**6, transcendentals=10**6),
    )(o_part, x.reshape(8, 16, DIM), gain[None, :], wo, wg, wu, wd)


def solution(mesh):
    def local_step(layer_in, new_pos, k_blk, v_blk, attn_gain, w_query, w_key, w_value, w_out, mlp_gain, w_gate, w_up, w_down):
        k_upd, v_upd, o_part, k_new, v_new = run_attn(
            new_pos, layer_in, attn_gain, w_query, w_key, w_value, k_blk, v_blk
        )
        y = run_tail(o_part, layer_in, mlp_gain, w_out, w_gate, w_up, w_down)
        shape = (ROWS, SLOTS, KVH, HD)
        new = (ROWS, KVH, HD)
        return y.reshape(ROWS, DIM), k_upd.reshape(shape), v_upd.reshape(shape), k_new.reshape(new), v_new.reshape(new)

    cache_spec = P('dp', 'sp', 'tp', None)
    new_spec = P('dp', 'tp', None)
    in_specs = (P('dp', None), P('dp'), cache_spec, cache_spec, P(None), P(None, 'tp'), P(None, 'tp'), P(None, 'tp'), P('tp', None), P(None), P(None, 'tp'), P(None, 'tp'), P('tp', None))
    out_specs = (P('dp', None), cache_spec, cache_spec, new_spec, new_spec)
    return jax.shard_map(local_step, mesh=mesh, in_specs=in_specs, out_specs=out_specs, check_vma=False)
```

time: 342 us -> 120 us (0.35)
  waiting for transfers between devices: 129 us -> 0 us
  matrix products: 114 us -> 0 us
  Pallas kernels: 0 us -> 113 us
  other arithmetic: 45.2 us -> 0 us
  blocking collectives: 34.9 us -> 0 us
  between operations: 13.9 us -> 0.65 us
    psum x3 -> x0, waiting for transfers between devices: 129 us -> none  [the longest x1 57.5 us: local_step(): lax.psum(jnp.dot(attn_vec, w_out, preferred_element_type=jnp.float32), 'tp')]
    dot_general x8 -> x0, matrix products: 114 us -> none  [the longest x1 41.3 us: local_step(): mlp_part = jnp.dot(act_bf, w_down, preferred_element_type=jnp.float32)]
    pallas_call x0 -> x2, Pallas kernels: none -> 113 us  [the longest x1 76 us: run_tail(): pl.pallas_call(tail_kernel, name='tail', out_shape=jax.ShapeDtypeStruct((...]
    select_n x1 -> x0, other arithmetic: 29.1 us -> none  [local_step(): k_upd = jnp.where(is_new, k_rot[:, None], k_blk)]
    psum x1 -> x0, blocking collectives: 17.6 us -> none  [local_step(): denom_sum = lax.psum(jnp.sum(prob_vals, axis=-1, keepdims=True), 'sp')]
    pmax x1 -> x0, blocking collectives: 17.3 us -> none  [local_step(): row_max = lax.pmax(jnp.max(scores, axis=-1, keepdims=True), 'sp')]
    convert_element_type x6 -> x0, other arithmetic: 6.43 us -> none  [the longest x1 2.88 us: local_step(): layer_out = (hidden + lax.psum(mlp_part, 'tp')).astype(jnp.bfloat16)]
    reduce_sum x3 -> x0, other arithmetic: 4.97 us -> none  [the longest x2 3.61 us: rms_norm(): mean_sq = jnp.mean(jnp.square(in_vec), axis=-1, keepdims=True)]
  transfers between devices with their start and end apart: 3 -> 0, of which waited for: 3 -> 0; matrix products, arithmetic and copies ran while one was open for 0% -> 0% of each run, Pallas kernels for 0% -> 0%
where the time goes in v1:
time: 120 us
  Pallas kernels  113 us (94%)
  local copies, waits for them, and re-layouts  6.3 us (5%)
    pallas_call x1, Pallas kernels, run_tail(): pl.pallas_call(tail_kernel, name='tail', out_shape=jax.ShapeDtypeStruct((...  76 us
    pallas_call x1, Pallas kernels, run_attn(): pl.pallas_call(attn_kernel, name='attn', out_shape=[cache, cache, jax.Sha...  36.7 us

profile of v1, /device:TPU:0, one launch (start us, length us, event | category | flops | bytes accessed | tf_op | source)
XLA Modules:
  0.0 119.6 jit_solution(9310864246569284031)
XLA Ops:
  0.6 1.3 %broadcast_in_dim.10.gain_ref = bf16[1,4096]{1,0:T(2,128)(2,1)} reshape(bf16[4096]{0:T(1024)(128)(2,1)} %param.18) | data formatting | bytes 16384 | tf_op jit(solution)/shard_map/broadcast_in_dim | solution.py:203
  1.9 1.3 %broadcast_in_dim.11.gain_ref = bf16[1,4096]{1,0:T(2,128)(2,1)} reshape(bf16[4096]{0:T(1024)(128)(2,1)} %param.23) | data formatting | bytes 16384 | tf_op jit(solution)/shard_map/broadcast_in_dim | solution.py:498
  3.3 1.4 %copy.19.pos_v = s32[128,1]{1,0:T(8,128)} copy(s32[128,1]{0,1:T(1,128)} %bitcast.13) | data formatting | bytes 1024 | tf_op jit(solution)/shard_map/broadcast_in_dim | solution.py:203
  4.6 36.7 %attn.1 = (bf16[128,512,128]{2,1,0:T(8,128)(2,1)}, bf16[128,512,128]{2,1,0:T(8,128)(2,1)}, f32[8,264,128]{2,1,0:T(8,128)}, bf16[512,128]{1,0:T(8,128)(2,1)}, bf16[512,128]{1,0:T(8,128)(2,1)}) custom-call(s32[128]{0:T(128)} %pos_s.1, bf16[128,4096]{1,0:T(8,128)(2,1)} %x_ref.1, s32[128,1]{1,0:T(8,128)} %copy.19.pos_v, f32[1,128]{1,0:T(1,128)} %constant.2.clone.freq_ref, ...), custom_call_target="tpu_custom_call" | custom-call | flops 4000000000 | bytes 92000000 | tf_op jit(solution)/shard_map/attn/pallas_call | solution.py:180
  41.4 76.0 %tail.1 = bf16[8,16,4096]{2,1,0:T(8,128)(2,1)} custom-call(f32[8,264,128]{2,1,0:T(8,128)} %get-tuple-element.10.o_in, bf16[8,16,4096]{2,1,0:T(8,128)(2,1)} %bitcast.11, bf16[1,4096]{1,0:T(2,128)(2,1)} %broadcast_in_dim.11.gain_ref, bf16[2048,4096]{1,0:T(8,128)(2,1)} %wo.1, bf16[4096,7168]{1,0:T(8,128)(2,1)} %wg.1, bf16[4096,7168]{1,0:T(8,128)(2,1)} %wu.1, ...), custom_call_target="tpu_custom_call" | custom-call | flops 6000000000 | bytes 62000000 | tf_op jit(solution)/shard_map/tail/pallas_call | solution.py:461
  117.4 2.3 %copy.21 = bf16[128,4096]{1,0:T(8,128)(2,1)} copy(bf16[128,4096]{1,0:T(8,128)(2,1)} %bitcast.12) | data formatting | bytes 2097152

commit v2 on v1

--- a/solution.py
+++ b/solution.py
@@ -28,9 +28,15 @@
 WRING = 3
 
 
-def rms(x, gain):
+def rms(x, gain_ref):
     ms = jnp.mean(jnp.square(x), axis=-1, keepdims=True)
-    return x * lax.rsqrt(ms + 1e-5) * gain.astype(F32)
+    gain = gain_ref[...].astype(F32)
+    gain = jnp.concatenate([gain[j : j + 1, :] for j in range(DIM // 128)], axis=1)
+    return x * lax.rsqrt(ms + 1e-5) * gain
+
+
+def column(v):
+    return jnp.transpose(jnp.broadcast_to(v, (128, 128)))
 
 
 def attn_kernel(
@@ -64,8 +70,8 @@
         for c in copies_in(i, i):
             c.start()
 
-    n_s[...] = rms(x_ref[...].astype(F32), gain_ref[...]).astype(BF16)
-    ang = pos_v[...].astype(F32) * freq_ref[...]
+    n_s[...] = rms(x_ref[...].astype(F32), gain_ref).astype(BF16)
+    ang = column(pos_v[...].astype(F32)) * freq_ref[...]
     lane = lax.broadcasted_iota(jnp.int32, (ROWS, HD), 1)
     even = (lane & 1) == 0
     cosr = jnp.cos(ang)
@@ -200,12 +206,14 @@
         compiler_params=pltpu.CompilerParams(vmem_limit_bytes=56 * MIB),
         cost_estimate=pl.CostEstimate(flops=4 * 10**9, bytes_accessed=92 * 10**6, transcendentals=10**6),
     )(
-        pos, x, pos[:, None], freq, gain[None, :], wq, wk, wv,
+        pos, x, pos[None, :], freq, gain.reshape(32, 128), wq, wk, wv,
         k_blk.reshape(ROWS, SLOTS * KVH, HD), v_blk.reshape(ROWS, SLOTS * KVH, HD),
     )
 
 
-NC = 8
+NG = 4
+GW = DIM // NG
+NC = 4
 CW = DIM // NC
 HC = CW // 2
 
@@ -252,9 +260,6 @@
     for c in (cx, cwo, cwg, cwu):
         c.start()
 
-    def column(v):
-        return jnp.transpose(jnp.broadcast_to(v, (128, 128)))
-
     def merge(a, b, put, last):
         m1, m2 = a[pl.ds(256, 2), :], b[pl.ds(256, 2), :]
         l1, l2 = a[pl.ds(258, 2), :], b[pl.ds(258, 2), :]
@@ -299,18 +304,18 @@
         obf[:, h * HD : (h + 1) * HD] = ofin[pl.ds(h, 32, stride=QH), :].astype(BF16)
 
     cwo.wait()
-    NY = 4
+    NY = 2
     YW = DIM // NY
     ycp = []
     for j in range(NY):
 
         def ostep(i, _):
-            cols = pl.ds(pl.multiple_of(j * YW + i * 512, 512), 512)
+            cols = pl.ds(pl.multiple_of(j * YW + i * 1024, 1024), 1024)
             v = jnp.dot(obf[...], wo_v[:, cols], preferred_element_type=F32)
-            wp[:, :, cols] = v.reshape(2, 16, 512)
+            wp[:, :, cols] = v.reshape(2, 16, 1024)
             return 0
 
-        lax.fori_loop(0, YW // 512, ostep, 0)
+        lax.fori_loop(0, YW // 1024, ostep, 0)
         cols = pl.ds(j * YW, YW)
         c = rc(wp.at[1 - yi, :, cols], ry.at[:, cols], ysem.at[j], dev_y)
         c.start()
@@ -321,7 +326,7 @@
         cols = pl.ds(j * YW, YW)
         ycp[j].wait_recv()
         hs[:, cols] = xs[:, cols].astype(F32) + wp[yi, :, cols] + ry[:, cols]
-    gat[me] = rms(hs[...], gain_ref[...]).astype(BF16).astype(F32)
+    gat[me] = rms(hs[...], gain_ref).astype(BF16).astype(F32)
 
     def gather0(buf, c0, w, sems):
         cs = pl.ds(c0, w)
@@ -354,28 +359,44 @@
         c.start()
         return [c]
 
-    g0 = gather0(gat, 0, DIM, gsem)
-    g1 = gather1(gat, 0, DIM, gsem, g0)
-    g2 = gather2(gat, 0, DIM, gsem, g1)
-    for c in (g0[2], g1[1], g1[3], g2[0]):
-        c.wait_recv()
-
-    def cast(r, _):
-        nbf[pl.ds(pl.multiple_of(r * 16, 16), 16), :] = gat[r].astype(BF16)
-        return 0
-
-    lax.fori_loop(0, 8, cast, 0)
+    g0 = [gather0(gat, j * GW, GW, gsem.at[j]) for j in range(NG)]
     cwg.wait()
     cwu.wait()
-
-    def up(i, _):
+    g1 = [gather1(gat, j * GW, GW, gsem.at[j], g0[j]) for j in range(NG)]
+    g2 = []
+
+    def up(j):
+        for c in (g0[j][2], g1[j][1], g1[j][3], g2[j][0]):
+            c.wait_recv()
+        ks = pl.ds(j * GW, GW)
+        for r in range(8):
+            nbf[pl.ds(r * 16, 16), :] = gat[r, :, ks].astype(BF16)
+
+        def step(i, _):
+            for w, base in ((wg_v, 0), (wu_v, HSL)):
+                v = jnp.dot(
+                    nbf[...], w[ks, pl.ds(pl.multiple_of(i * 256, 256), 256)], preferred_element_type=F32
+                ).reshape(8, 16, 256)
+                cols = pl.ds(pl.multiple_of(base + i * 256, 256), 256)
+                part[:, :, cols] = v if j == 0 else part[:, :, cols] + v
+            return 0
+
+        lax.fori_loop(0, HSL // 256, step, 0)
+
+    for j in range(NG):
+        g2.append(gather2(gat, j * GW, GW, gsem.at[j], g1[j]))
+        if j:
+            up(j - 1)
+    up(NG - 1)
+
+    def gate(i, _):
         cols = pl.ds(pl.multiple_of(i * 256, 256), 256)
-        g = jnp.dot(nbf[...], wg_v[:, cols], preferred_element_type=F32)
-        u = jnp.dot(nbf[...], wu_v[:, cols], preferred_element_type=F32)
+        g = part[:, :, cols].reshape(ROWS, 256)
+        u = part[:, :, pl.ds(pl.multiple_of(HSL + i * 256, 256), 256)].reshape(ROWS, 256)
         act[:, cols] = (jax.nn.silu(g) * u).astype(BF16)
         return 0
 
-    lax.fori_loop(0, HSL // 256, up, 0)
+    lax.fori_loop(0, HSL // 256, gate, 0)
     cwd.wait()
 
     state = [dict() for _ in range(NC)]
@@ -440,15 +461,18 @@
             c.wait_recv()
         out_ref[:, :, cs] = gat2[:, :, cs].astype(BF16)
 
-    stages = (s0, s1, s2, s3, s4, s5, s6)
-    for t in range(NC + len(stages) - 1):
-        for k, stage in enumerate(stages):
-            if 0 <= t - k < NC:
-                stage(t - k)
+    for t in range(NC + 1):
+        if t < NC:
+            s0(t)
+        if t:
+            s1(t - 1)
+    for stage in (s2, s3, s4, s5, s6):
+        for j in range(NC):
+            stage(j)
 
     b1.wait_send()
     b2.wait_send()
-    for c in ycp + g0 + g1 + g2:
+    for c in ycp + sum(g0 + g1 + g2, []):
         c.wait_send()
     for st in state:
         for c in st["r"] + [st["r2"]] + st["g0"] + st["g1"] + st["g2"]:
@@ -478,7 +502,7 @@
             pltpu.VMEM((16, DIM), F32),
             pltpu.VMEM((16, DIM), BF16),
             pltpu.VMEM((8, 16, DIM), F32),
-            pltpu.VMEM((ROWS, DIM), BF16),
+            pltpu.VMEM((ROWS, GW), BF16),
             pltpu.VMEM((ROWS, HSL), BF16),
             pltpu.VMEM((8, 16, DIM), F32),
             pltpu.VMEM((4, 16, DIM), F32),
@@ -487,15 +511,15 @@
             pltpu.VMEM((8, 16, DIM), F32),
             pltpu.SemaphoreType.DMA((5,)),
             pltpu.SemaphoreType.DMA((2, 2)),
-            pltpu.SemaphoreType.DMA((4, 2)),
-            pltpu.SemaphoreType.DMA((8, 2)),
+            pltpu.SemaphoreType.DMA((2, 2)),
+            pltpu.SemaphoreType.DMA((NG, 8, 2)),
             pltpu.SemaphoreType.DMA((NC, 12, 2)),
         ],
         compiler_params=pltpu.CompilerParams(
             collective_id=0, has_side_effects=True, vmem_limit_bytes=67043328
         ),
         cost_estimate=pl.CostEstimate(flops=6 * 10**9, bytes_accessed=62 * 10**6, transcendentals=10**6),
-    )(o_part, x.reshape(8, 16, DIM), gain[None, :], wo, wg, wu, wd)
+    )(o_part, x.reshape(8, 16, DIM), gain.reshape(32, 128), wo, wg, wu, wd)
 
 
 def solution(mesh):

time: 120 us -> 110 us (0.917)
  Pallas kernels: 113 us -> 107 us
  local copies, waits for them, and re-layouts: 6.3 us -> 2.29 us
    pallas_call x1, Pallas kernels: 76 us -> 69.9 us  [run_tail(): pl.pallas_call(tail_kernel, name='tail', out_shape=jax.ShapeDtypeStruct((...]
    broadcast_in_dim x3 -> x0, local copies, waits for them, and re-layouts: 4.01 us -> none  [the longest x1 1.39 us: run_attn(): pos[:, None]]
where the time goes in v2:
time: 110 us
  Pallas kernels  107 us (97%)
  local copies, waits for them, and re-layouts  2.29 us (2%)
    pallas_call x1, Pallas kernels, run_tail(): pl.pallas_call(tail_kernel, name='tail', out_shape=jax.ShapeDtypeStruct((...  69.9 us
    pallas_call x1, Pallas kernels, run_attn(): pl.pallas_call(attn_kernel, name='attn', out_shape=[cache, cache, jax.Sha...  36.7 us
    unnamed x1, local copies, waits for them, and re-layouts  2.29 us

profile of v2, /device:TPU:0, one launch (start us, length us, event | category | flops | bytes accessed | tf_op | source)
XLA Modules:
  0.0 109.6 jit_solution(4681615532769019043)
XLA Ops:
  0.6 36.7 %attn.1 = (bf16[128,512,128]{2,1,0:T(8,128)(2,1)}, bf16[128,512,128]{2,1,0:T(8,128)(2,1)}, f32[8,264,128]{2,1,0:T(8,128)}, bf16[512,128]{1,0:T(8,128)(2,1)}, bf16[512,128]{1,0:T(8,128)(2,1)}) custom-call(s32[128]{0:T(128)} %pos_s.1, bf16[128,4096]{1,0:T(8,128)(2,1)} %x_ref.1, s32[1,128]{1,0:T(1,128)} %bitcast.17, f32[1,128]{1,0:T(1,128)} %constant.2.clone.freq_ref, ...), custom_call_target="tpu_custom_call" | custom-call | flops 4000000000 | bytes 92000000 | tf_op jit(solution)/shard_map/attn/pallas_call | solution.py:186
  37.4 69.9 %tail.1 = bf16[8,16,4096]{2,1,0:T(8,128)(2,1)} custom-call(f32[8,264,128]{2,1,0:T(8,128)} %get-tuple-element.10.o_in, bf16[8,16,4096]{2,1,0:T(8,128)(2,1)} %bitcast.13, bf16[32,128]{1,0:T(8,128)(2,1)} %bitcast.16, bf16[2048,4096]{1,0:T(8,128)(2,1)} %wo.1, bf16[4096,7168]{1,0:T(8,128)(2,1)} %wg.1, bf16[4096,7168]{1,0:T(8,128)(2,1)} %wu.1, bf16[7168,4096]{1,0:T(8,128)(2,1)} %wd.1), custom_call_target="tpu_custom_call" | custom-call | flops 6000000000 | bytes 62000000 | tf_op jit(solution)/shard_map/tail/pallas_call | solution.py:485
  107.3 2.3 %copy.20 = bf16[128,4096]{1,0:T(8,128)(2,1)} copy(bf16[128,4096]{1,0:T(8,128)(2,1)} %bitcast.14) | data formatting | bytes 2097152

commit v3 on v2

v3 whole, which is shorter than its diff:
```python
import functools

import jax
import jax.numpy as jnp
import numpy as np
from jax import lax
from jax.experimental import pallas as pl
from jax.experimental.pallas import tpu as pltpu
from jax.sharding import PartitionSpec as P

ROPE_THETA = 1000000
MESH = pl.DeviceIdType.MESH
F32 = jnp.float32
BF16 = jnp.bfloat16
MIB = 2**20

ROWS = 128
DIM = 4096
HD = 128
SLOTS = 128
KVH = 4
QH = 16
HID = 7168
HSL = HID // 4
NEG = -1e30
PAIR = 2
M_AT = pl.ds(256, PAIR)
L_AT = pl.ds(258, PAIR)
RING = 4

def rms(x, gain_ref):
    ms = jnp.mean(jnp.square(x), axis=-1, keepdims=True)
    gain = gain_ref[...].astype(F32)
    gain = jnp.concatenate([gain[j : j + 1, :] for j in range(DIM // 128)], axis=1)
    return x * lax.rsqrt(ms + 1e-5) * gain


def column(v):
    return jnp.transpose(jnp.broadcast_to(v, (128, 128)))


def place():
    sp = lax.axis_index("sp")
    yi = lax.axis_index("tp")
    dp = lax.axis_index("dp")
    core = lax.rem(sp, 2)
    xi = sp // 2
    oc = 1 - core
    ox = 1 - xi
    return sp, yi, core, xi, oc, ox, (dp, yi, 2 * xi + oc), (dp, yi, 2 * ox + core), (dp, 1 - yi, sp)


def block_of(c, x, y):
    return 4 * c + 2 * x + y


def rc(src, dst, sems, dev):
    return pltpu.make_async_remote_copy(
        src_ref=src, dst_ref=dst, send_sem=sems.at[0], recv_sem=sems.at[1],
        device_id=dev, device_id_type=MESH,
    )


def front_kernel(
    pos_s, x_ref, pos_v, freq_ref, gain_ref, wq, wk, wv, wo, k_in, v_in,
    kn_out, vn_out, kdup, vdup, own_out, oth_out,
    n_s, wbuf, kbuf, vbuf, qraw, kvraw, qf, slotb, o_s, rba, rbb, rbx, ob, ofin, obf,
    wsem, isem, qsem, bsem,
):
    sp, yi, core, xi, oc, ox, dev_c, dev_x, dev_y = place()

    bar = pltpu.get_barrier_semaphore()
    for dev in (dev_c, dev_x):
        pl.semaphore_signal(bar, inc=1, device_id=dev, device_id_type=MESH)

    def row_block(t):
        p, y = t // 2, t % 2
        c = core + (oc - core) * (1 - p % 2)
        x = xi + (ox - xi) * (1 - p // 2)
        return block_of(c, x, y)

    def cache_copies(t):
        rows = pl.ds(row_block(t) * 16, 16)
        return (
            pltpu.make_async_copy(k_in.at[rows], kbuf.at[t % RING], isem.at[0, t % RING]),
            pltpu.make_async_copy(v_in.at[rows], vbuf.at[t % RING], isem.at[1, t % RING]),
        )

    def cols(start, width):
        return pl.ds(pl.multiple_of(start, 128), width)

    wcp = [
        [
            pltpu.make_async_copy(wk.at[:, cols(core * 256, 256)], wbuf.at[0, :, pl.ds(0, 256)], wsem.at[0]),
            pltpu.make_async_copy(wv.at[:, cols(core * 256, 256)], wbuf.at[0, :, pl.ds(256, 256)], wsem.at[1]),
        ],
        [pltpu.make_async_copy(wq.at[:, cols(core * 1024, 512)], wbuf.at[1], wsem.at[2])],
        [pltpu.make_async_copy(wq.at[:, cols(core * 1024 + 512, 512)], wbuf.at[2], wsem.at[3])],
    ]
    ocp = [
        pltpu.make_async_copy(
            wo.at[:, pl.ds(512 * i, 512)], wbuf.at[i // 2, pl.ds(2048 * (i % 2), 2048)], wsem.at[4 + i]
        )
        for i in range(8)
    ]
    for group in wcp:
        for c in group:
            c.start()
    for c in cache_copies(0):
        c.start()

    n_s[...] = rms(x_ref[...].astype(F32), gain_ref).astype(BF16)
    ang = column(pos_v[...].astype(F32)) * freq_ref[...]
    lane = lax.broadcasted_iota(jnp.int32, (ROWS, HD), 1)
    even = (lane & 1) == 0
    cosr = jnp.cos(ang)
    sinr = jnp.sin(ang)
    sinr = jnp.where(even, -sinr, sinr)
    slotb[...] = (lax.broadcasted_iota(jnp.int32, (SLOTS * KVH, HD), 0) >> 2).astype(F32).astype(BF16)

    def rotate(y):
        swap = jnp.where(even, pltpu.roll(y, HD - 1, 1), pltpu.roll(y, 1, 1))
        return y * cosr + swap * sinr

    qcp = []
    for j in range(3):
        for c in wcp[j]:
            c.wait()
        y = jnp.dot(n_s[...], wbuf[j], preferred_element_type=F32)
        for c in cache_copies(1 + j):
            c.start()
        for hh in range(4):
            yh = y[:, hh * HD : (hh + 1) * HD]
            if j == 0 and hh < 2:
                kvraw[0, 2 * core + hh] = rotate(yh)
            elif j == 0:
                kvraw[1, 2 * core + hh - 2] = yh
            else:
                qraw[8 * core + (j - 1) * 4 + hh] = rotate(yh)
        if j == 0:
            pl.semaphore_wait(bar, 2)
            for i in range(PAIR):
                ref = kvraw.at[i, pl.ds(2 * core, 2)]
                qcp.append(rc(ref, ref, qsem.at[i], dev_c))
        else:
            ref = qraw.at[pl.ds(8 * core + (j - 1) * 4, 4)]
            qcp.append(rc(ref, ref, qsem.at[1 + j], dev_c))
            if j == 1:
                qcp[0].start()
                qcp[1].start()
                qcp[2].start()
            else:
                qcp[3].start()
    for c in qcp:
        c.wait_recv()
    for i, (dup, out) in enumerate(((kdup, kn_out), (vdup, vn_out))):
        for h in range(KVH):
            v = kvraw[i, h]
            ofin[pl.ds(h, ROWS, stride=KVH), :] = v
            for rep in range(PAIR):
                dup[pl.ds(rep * KVH + h, ROWS, stride=8), :] = v
        out[...] = ofin[...].astype(BF16)
    for h in range(QH):
        qf[pl.ds(h, ROWS, stride=QH), :] = qraw[h]

    col = lax.broadcasted_iota(jnp.int32, (QH, SLOTS * KVH), 1)
    hrow = lax.broadcasted_iota(jnp.int32, (QH, SLOTS * KVH), 0)
    slot_id = jnp.where((col & 3) == (hrow >> 2), col >> 2, jnp.int32(1 << 20))
    eye = lax.broadcasted_iota(jnp.int32, (128, 128), 0) == lax.broadcasted_iota(
        jnp.int32, (128, 128), 1
    )

    def merge(a, b, put, last):
        m1, m2 = a[M_AT, :], b[M_AT, :]
        l1, l2 = a[L_AT, :], b[L_AT, :]
        m = jnp.maximum(m1, m2)
        a1 = jnp.exp(m1 - m)
        a2 = jnp.exp(m2 - m)
        l = a1 * l1 + a2 * l2
        if last:
            a1 = a1 / l
            a2 = a2 / l
        for g in range(PAIR):
            rows = pl.ds(g * 128, 128)
            put(g, column(a1[g : g + 1]) * a[rows, :] + column(a2[g : g + 1]) * b[rows, :])
        return m, l

    def merge_into(dst, a, b):
        def put(g, v):
            dst[pl.ds(g * 128, 128), :] = v

        m, l = merge(a, b, put, False)
        dst[M_AT, :] = m
        dst[L_AT, :] = l

    pair = {
        "a": block_of(oc, ox, 0),
        "x": block_of(core, ox, 0),
        "b": block_of(oc, xi, 0),
        "own": block_of(core, xi, 0),
    }
    send_a = rc(o_s.at[pl.ds(pair["a"], 2)], rba, bsem.at[0], dev_c)
    send_b = rc(o_s.at[pl.ds(pair["b"], 2)], rbb, bsem.at[1], dev_c)
    send_x = rc(ob.at[pl.ds(0, 2)], rbx, bsem.at[2], dev_x)

    def block(t, _):
        r = row_block(t)
        for c in cache_copies(t):
            c.wait()

        @pl.when(t == 4)
        def _():
            for c in ocp:
                c.start()

        for half in range(PAIR):
            sc, lims, vals = [], [], []
            for b in range(8):
                row = r * 16 + half * 8 + b
                lim = pos_s[row] - sp * SLOTS
                lims.append(lim)
                hit = slotb[...] == lax.broadcast(lim.astype(F32), (SLOTS * KVH, HD)).astype(BF16)
                new = pl.ds(pl.multiple_of(row * 8, 8), 8)
                kv = []
                for dup, ref in ((kdup, kbuf), (vdup, vbuf)):
                    d = dup[new, :]
                    d = jnp.concatenate([d, d], axis=0).astype(BF16)
                    d = jnp.concatenate([d] * 32, axis=0)
                    kv.append(jnp.where(hit, d, ref[t % RING, half * 8 + b]))
                vals.append(kv[1])
                q = qf[pl.ds(pl.multiple_of(row * QH, QH), QH), :].astype(BF16)
                sc.append(
                    lax.dot_general(
                        q, kv[0], (((1,), (1,)), ((), ())), preferred_element_type=F32
                    )
                )
            ms, ls = [], []
            for b in range(8):
                ok = slot_id <= lims[b]
                s = jnp.where(ok, sc[b] * (HD**-0.5), NEG)
                m = jnp.maximum(jnp.max(s, axis=-1, keepdims=True), NEG * 0.1)
                w = jnp.exp(s - m)
                ms.append(m)
                ls.append(jnp.sum(w, axis=-1, keepdims=True))
                o = jnp.dot(w.astype(BF16), vals[b], preferred_element_type=F32)
                o_s[r, pl.ds((half * 8 + b) * QH, QH), :] = o
            m = jnp.concatenate(ms, axis=0)
            l = jnp.concatenate(ls, axis=0)
            o_s[r, pl.ds(256 + half, 1), :] = jnp.sum(jnp.where(eye, m, 0.0), axis=0, keepdims=True)
            o_s[r, pl.ds(258 + half, 1), :] = jnp.sum(jnp.where(eye, l, 0.0), axis=0, keepdims=True)

        @pl.when(t == 1)
        def _():
            send_a.start()

        @pl.when(t == 3)
        def _():
            send_a.wait_recv()
            for q in range(PAIR):
                merge_into(ob.at[q], o_s.at[pair["x"] + q], rba.at[q])
            send_x.start()

        @pl.when(t == 5)
        def _():
            send_b.start()

        @pl.when(t < 8 - RING)
        def _():
            for c in cache_copies(t + RING):
                c.start()

        return 0

    lax.fori_loop(0, 8, block, 0)
    send_b.wait_recv()
    for q in range(PAIR):
        merge_into(ob.at[2 + q], o_s.at[pair["own"] + q], rbb.at[q])
    send_x.wait_recv()
    for q in range(PAIR):

        def put(g, v):
            ofin[pl.ds(q * 256 + g * 128, 128), :] = v

        merge(ob.at[2 + q], rbx.at[q], put, True)
    for h in range(QH):
        obf[:, h * HD : (h + 1) * HD] = ofin[pl.ds(h, 32, stride=QH), :].astype(BF16)

    for c in ocp:
        c.wait()
    for i in range(4):
        v = jnp.concatenate(
            [
                jnp.dot(obf[...], wbuf[i, 2048 * k : 2048 * (k + 1), :], preferred_element_type=F32)
                for k in range(PAIR)
            ],
            axis=1,
        )
        cs = pl.ds(i * 1024, 1024)
        own_out[:, cs] = jnp.where(yi == 0, v[:16], v[16:])
        oth_out[:, cs] = jnp.where(yi == 0, v[16:], v[:16])
    for c in qcp + [send_a, send_b, send_x]:
        c.wait_send()


def run_front(pos, x, gain, wq, wk, wv, wo, k_blk, v_blk):
    half_idx = np.arange(HD // 2, dtype=np.float32)
    inv = (1.0 / np.power(np.float32(ROPE_THETA), np.float32(2.0) * half_idx / np.float32(HD))).astype(np.float32)
    freq = jnp.asarray(np.repeat(inv, 2)[None, :])
    vm = pl.BlockSpec(memory_space=pltpu.VMEM)
    hbm = pl.BlockSpec(memory_space=pl.ANY)
    ring = pltpu.VMEM((RING, 16, SLOTS * KVH, HD), BF16)
    dup = jax.ShapeDtypeStruct((ROWS * 8, HD), F32)
    new = jax.ShapeDtypeStruct((ROWS * KVH, HD), BF16)
    rows = jax.ShapeDtypeStruct((16, DIM), F32)
    part = pltpu.VMEM((2, 264, 128), F32)
    return pl.pallas_call(
        front_kernel,
        name="front",
        out_shape=[new, new, dup, dup, rows, rows],
        in_specs=[pl.BlockSpec(memory_space=pltpu.SMEM), vm, vm, vm, vm] + [hbm] * 6,
        out_specs=[vm] * 6,
        scratch_shapes=[
            pltpu.VMEM((ROWS, DIM), BF16),
            pltpu.VMEM((4, DIM, 512), BF16),
            ring,
            ring,
            pltpu.VMEM((QH, ROWS, HD), F32),
            pltpu.VMEM((2, KVH, ROWS, HD), F32),
            pltpu.VMEM((ROWS * QH, HD), F32),
            pltpu.VMEM((SLOTS * KVH, HD), BF16),
            pltpu.VMEM((8, 264, 128), F32),
            part,
            part,
            part,
            pltpu.VMEM((4, 264, 128), F32),
            pltpu.VMEM((512, 128), F32),
            pltpu.VMEM((32, 2048), BF16),
            pltpu.SemaphoreType.DMA((12,)),
            pltpu.SemaphoreType.DMA((2, RING)),
            pltpu.SemaphoreType.DMA((4, 2)),
            pltpu.SemaphoreType.DMA((3, 2)),
        ],
        compiler_params=pltpu.CompilerParams(
            collective_id=1, has_side_effects=True, vmem_limit_bytes=56 * MIB
        ),
        cost_estimate=pl.CostEstimate(flops=4 * 10**9, bytes_accessed=63 * 10**6, transcendentals=10**6),
    )(
        pos, x, pos[None, :], freq, gain.reshape(32, 128), wq, wk, wv, wo,
        k_blk.reshape(ROWS, SLOTS * KVH, HD), v_blk.reshape(ROWS, SLOTS * KVH, HD),
    )


def write_kernel(pos_s, kdup, vdup, kn, vn, k_in, v_in, k_out, v_out, kn_out, vn_out, tok, kbuf, vbuf, isem, osem):
    sp = lax.axis_index("sp")

    def copies_in(i, s):
        rows = pl.ds(i * WROWS, WROWS)
        return (
            pltpu.make_async_copy(k_in.at[rows], kbuf.at[s], isem.at[0, s]),
            pltpu.make_async_copy(v_in.at[rows], vbuf.at[s], isem.at[1, s]),
        )

    def copies_out(i, s):
        rows = pl.ds(i * WROWS, WROWS)
        return (
            pltpu.make_async_copy(kbuf.at[s], k_out.at[rows], osem.at[0, s]),
            pltpu.make_async_copy(vbuf.at[s], v_out.at[rows], osem.at[1, s]),
        )

    for i in range(WSTEPS):
        for c in copies_in(i, i):
            c.start()
    kn_out[...] = kn[...]
    vn_out[...] = vn[...]
    tok[...] = jnp.zeros_like(tok)
    r16 = lax.broadcasted_iota(jnp.int32, (16, HD), 0) >> 2

    def block(r, _):
        s = r
        for c in copies_in(r, s):
            c.wait()
        for b in range(WROWS):
            row = r * WROWS + b
            lim = pos_s[row] - sp * SLOTS
            cl = jnp.clip(lim, 0, SLOTS - 1)
            at = pl.ds(pl.multiple_of((cl >> 2) * 16, 16), 16)
            hit = r16 == jnp.where(lim == cl, cl & 3, -1)
            new = pl.ds(pl.multiple_of(row * 8, 8), 8)
            for dup, buf in ((kdup, kbuf), (vdup, vbuf)):
                d = dup[new, :]
                d = jnp.concatenate([d, d], axis=0).astype(BF16)
                buf[s, b, at, :] = jnp.where(hit, d, buf[s, b, at, :])
        return 0

    lax.fori_loop(0, WSTEPS, block, 0)
    for i in range(WSTEPS):
        for c in copies_out(i, i):
            c.start()
    for i in range(WSTEPS):
        for c in copies_out(i, i):
            c.wait()


def run_write(pos, kdup, vdup, kn, vn, k_blk, v_blk):
    vm = pl.BlockSpec(memory_space=pltpu.VMEM)
    hbm = pl.BlockSpec(memory_space=pl.ANY)
    cache = jax.ShapeDtypeStruct((ROWS, SLOTS * KVH, HD), BF16)
    new = jax.ShapeDtypeStruct((ROWS * KVH, HD), BF16)
    ring = pltpu.VMEM((WSTEPS, WROWS, SLOTS * KVH, HD), BF16)
    return pl.pallas_call(
        write_kernel,
        name="write",
        out_shape=[cache, cache, new, new, jax.ShapeDtypeStruct((8, 128), F32)],
        in_specs=[pl.BlockSpec(memory_space=pltpu.SMEM), vm, vm, vm, vm, hbm, hbm],
        out_specs=[hbm, hbm, vm, vm, vm],
        scratch_shapes=[
            ring,
            ring,
            pltpu.SemaphoreType.DMA((2, WSTEPS)),
            pltpu.SemaphoreType.DMA((2, WSTEPS)),
        ],
        compiler_params=pltpu.CompilerParams(vmem_limit_bytes=56 * MIB),
        cost_estimate=pl.CostEstimate(flops=5 * 10**9, bytes_accessed=67 * 10**6, transcendentals=0),
    )(
        pos, kdup, vdup, kn, vn,
        k_blk.reshape(ROWS, SLOTS * KVH, HD), v_blk.reshape(ROWS, SLOTS * KVH, HD),
    )


WROWS = 16
WSTEPS = ROWS // WROWS
NG = 4
GW = DIM // NG
TAIL_VMEM = 62 * MIB + MIB // 2
NC = 4
CW = DIM // NC
HC = CW // 2


def tail_kernel(
    own_in, oth_in, x_in, gain_ref, wg, wu, wd, tok,
    out_ref,
    wd_v, wg_v, wu_v, hs, xs, gat, nbf, act,
    part, rd, r1, r2, gat2, wsem, gsem, fsem,
):
    del tok
    sp, yi, core, xi, oc, ox, dev_c, dev_x, dev_y = place()
    oy = 1 - yi
    me, me_x, me_y, me_xy = (block_of(core, a, b) for a, b in ((xi, yi), (ox, yi), (xi, oy), (ox, oy)))

    bar = pltpu.get_barrier_semaphore()
    for dev in (dev_c, dev_x, dev_y):
        pl.semaphore_signal(bar, inc=1, device_id=dev, device_id_type=MESH)

    hcols = pl.ds(pl.multiple_of(sp * HSL, 128), HSL)
    cx = pltpu.make_async_copy(x_in.at[me], xs, wsem.at[0])
    cx.start()
    cup = []
    for j in range(NG):
        ks = pl.ds(j * GW, GW)
        cup.append(
            [
                pltpu.make_async_copy(wg.at[ks, hcols], wg_v.at[ks], wsem.at[2 + 2 * j]),
                pltpu.make_async_copy(wu.at[ks, hcols], wu_v.at[ks], wsem.at[3 + 2 * j]),
            ]
        )
        for c in cup[j]:
            c.start()
    cwd = pltpu.make_async_copy(wd.at[hcols], wd_v, wsem.at[1])
    cwd.start()
    cx.wait()
    hs[...] = xs[...].astype(F32) + (own_in[...] + oth_in[...])
    gat[me] = rms(hs[...], gain_ref).astype(BF16).astype(F32)
    pl.semaphore_wait(bar, 3)

    def gather0(buf, c0, w, sems):
        cs = pl.ds(c0, w)
        out = []
        for k, dev in ((0, dev_x), (1, dev_y), (2, dev_c)):
            c = rc(buf.at[me, :, cs], buf.at[me, :, cs], sems.at[k], dev)
            c.start()
            out.append(c)
        return out

    def gather1(buf, c0, w, sems, cps):
        lo, hi, cs = pl.ds(c0, w // 2), pl.ds(c0 + w // 2, w // 2), pl.ds(c0, w)
        cps[0].wait_recv()
        a = rc(buf.at[me_x, :, lo], buf.at[me_x, :, lo], sems.at[3], dev_y)
        a.start()
        b = rc(buf.at[me_x, :, cs], buf.at[me_x, :, cs], sems.at[4], dev_c)
        b.start()
        cps[1].wait_recv()
        c = rc(buf.at[me_y, :, hi], buf.at[me_y, :, hi], sems.at[5], dev_x)
        c.start()
        d = rc(buf.at[me_y, :, cs], buf.at[me_y, :, cs], sems.at[6], dev_c)
        d.start()
        return [a, b, c, d]

    def gather2(buf, c0, w, sems, cps):
        cs = pl.ds(c0, w)
        cps[0].wait_recv()
        cps[2].wait_recv()
        c = rc(buf.at[me_xy, :, cs], buf.at[me_xy, :, cs], sems.at[7], dev_c)
        c.start()
        return [c]

    g0 = [gather0(gat, j * GW, GW, gsem.at[j]) for j in range(NG)]
    g1 = [gather1(gat, j * GW, GW, gsem.at[j], g0[j]) for j in range(NG)]
    g2 = []

    def up(j):
        for c in (g0[j][2], g1[j][1], g1[j][3], g2[j][0]):
            c.wait_recv()
        ks = pl.ds(j * GW, GW)
        for r in range(8):
            nbf[pl.ds(r * 16, 16), :] = gat[r, :, ks].astype(BF16)

        for c in cup[j]:
            c.wait()
        for w, base in ((wg_v, 0), (wu_v, HSL)):
            v = jnp.dot(nbf[...], w[ks, :], preferred_element_type=F32).reshape(8, 16, HSL)
            cols = pl.ds(base, HSL)
            part[:, :, cols] = v if j == 0 else part[:, :, cols] + v

    for j in range(NG):
        g2.append(gather2(gat, j * GW, GW, gsem.at[j], g1[j]))
        if j:
            up(j - 1)
    up(NG - 1)

    def gate(i, _):
        cols = pl.ds(pl.multiple_of(i * 256, 256), 256)
        g = part[:, :, cols].reshape(ROWS, 256)
        u = part[:, :, pl.ds(pl.multiple_of(HSL + i * 256, 256), 256)].reshape(ROWS, 256)
        act[:, cols] = (jax.nn.silu(g) * u).astype(BF16)
        return 0

    lax.fori_loop(0, HSL // 256, gate, 0)
    cwd.wait()

    state = [dict() for _ in range(NC)]

    def s0(j):
        cs = pl.ds(j * CW, CW)
        v = jnp.dot(act[...], wd_v[:, cs], preferred_element_type=F32)
        part[:, :, cs] = v.reshape(8, 16, CW)
        c = rc(part.at[pl.ds(4 * oc, 4), :, cs], rd.at[:, :, cs], fsem.at[j, 8], dev_c)
        c.start()
        state[j]["d"] = c

    def s1(j):
        cs = pl.ds(j * CW, CW)
        state[j]["d"].wait()
        mine = pl.ds(4 * core, 4)
        rd[:, :, cs] = part[mine, :, cs] + rd[:, :, cs]
        if j % 2 == 0:
            c = [rc(rd.at[pl.ds(2 * ox, 2), :, cs], r1.at[:, :, cs], fsem.at[j, 9], dev_x)]
        else:
            c = [
                rc(rd.at[2 * i + oy, :, cs], r1.at[i, :, cs], fsem.at[j, 9 + i], dev_y)
                for i in range(PAIR)
            ]
        for k in c:
            k.start()
        state[j]["r"] = c

    def s2(j):
        cs = pl.ds(j * CW, CW)
        for k in state[j]["r"]:
            k.wait_recv()
        if j % 2 == 0:
            for i in range(PAIR):
                r1[i, :, cs] = r1[i, :, cs] + rd[2 * xi + i, :, cs]
            c = rc(r1.at[oy, :, cs], r2.at[:, cs], fsem.at[j, 11], dev_y)
        else:
            for i in range(PAIR):
                r1[i, :, cs] = r1[i, :, cs] + rd[2 * i + yi, :, cs]
            c = rc(r1.at[ox, :, cs], r2.at[:, cs], fsem.at[j, 11], dev_x)
        c.start()
        state[j]["r2"] = c

    def s3(j):
        cs = pl.ds(j * CW, CW)
        state[j]["r2"].wait_recv()
        own = r1[yi, :, cs] if j % 2 == 0 else r1[xi, :, cs]
        y = hs[:, cs] + (own + r2[:, cs])
        gat2[me, :, cs] = y.astype(BF16).astype(F32)
        state[j]["g0"] = gather0(gat2, j * CW, CW, fsem.at[j])

    def s4(j):
        state[j]["g1"] = gather1(gat2, j * CW, CW, fsem.at[j], state[j]["g0"])

    def s5(j):
        state[j]["g2"] = gather2(gat2, j * CW, CW, fsem.at[j], state[j]["g1"])

    def s6(j):
        cs = pl.ds(j * CW, CW)
        st = state[j]
        for c in (st["g0"][2], st["g1"][1], st["g1"][3], st["g2"][0]):
            c.wait_recv()
        out_ref[:, :, cs] = gat2[:, :, cs].astype(BF16)

    for t in range(NC + 1):
        if t < NC:
            s0(t)
        if t:
            s1(t - 1)
    for stage in (s2, s3, s4, s5, s6):
        for j in range(NC):
            stage(j)

    for c in sum(g0 + g1 + g2, []):
        c.wait_send()
    for st in state:
        for c in st["r"] + [st["r2"]] + st["g0"] + st["g1"] + st["g2"]:
            c.wait_send()


def run_tail(own, oth, x, gain, wg, wu, wd, tok):
    vm = pl.BlockSpec(memory_space=pltpu.VMEM)
    hbm = pl.BlockSpec(memory_space=pl.ANY)
    return pl.pallas_call(
        tail_kernel,
        name="tail",
        out_shape=pltpu.VMEM((8, 16, DIM), BF16),
        in_specs=[vm, vm, hbm, vm, hbm, hbm, hbm, hbm],
        out_specs=vm,
        scratch_shapes=[
            pltpu.VMEM((HSL, DIM), BF16),
            pltpu.VMEM((DIM, HSL), BF16),
            pltpu.VMEM((DIM, HSL), BF16),
            pltpu.VMEM((16, DIM), F32),
            pltpu.VMEM((16, DIM), BF16),
            pltpu.VMEM((8, 16, DIM), F32),
            pltpu.VMEM((ROWS, GW), BF16),
            pltpu.VMEM((ROWS, HSL), BF16),
            pltpu.VMEM((8, 16, DIM), F32),
            pltpu.VMEM((4, 16, DIM), F32),
            pltpu.VMEM((2, 16, DIM), F32),
            pltpu.VMEM((16, DIM), F32),
            pltpu.VMEM((8, 16, DIM), F32),
            pltpu.SemaphoreType.DMA((2 + 2 * NG,)),
            pltpu.SemaphoreType.DMA((NG, 8, 2)),
            pltpu.SemaphoreType.DMA((NC, 12, 2)),
        ],
        compiler_params=pltpu.CompilerParams(
            collective_id=0, has_side_effects=True, vmem_limit_bytes=TAIL_VMEM
        ),
        cost_estimate=pl.CostEstimate(flops=6 * 10**9, bytes_accessed=62 * 10**6, transcendentals=10**6),
    )(own, oth, x.reshape(8, 16, DIM), gain.reshape(32, 128), wg, wu, wd, tok)


def solution(mesh):
    def local_step(layer_in, new_pos, k_blk, v_blk, attn_gain, w_query, w_key, w_value, w_out, mlp_gain, w_gate, w_up, w_down):
        kn, vn, kdup, vdup, own, oth = run_front(
            new_pos, layer_in, attn_gain, w_query, w_key, w_value, w_out, k_blk, v_blk
        )
        oth = lax.ppermute(oth, 'tp', [(0, 1), (1, 0)])
        k_upd, v_upd, k_new, v_new, tok = run_write(new_pos, kdup, vdup, kn, vn, k_blk, v_blk)
        y = run_tail(own, oth, layer_in, mlp_gain, w_gate, w_up, w_down, tok)
        shape = (ROWS, SLOTS, KVH, HD)
        new = (ROWS, KVH, HD)
        return y.reshape(ROWS, DIM), k_upd.reshape(shape), v_upd.reshape(shape), k_new.reshape(new), v_new.reshape(new)

    cache_spec = P('dp', 'sp', 'tp', None)
    new_spec = P('dp', 'tp', None)
    in_specs = (P('dp', None), P('dp'), cache_spec, cache_spec, P(None), P(None, 'tp'), P(None, 'tp'), P(None, 'tp'), P('tp', None), P(None), P(None, 'tp'), P(None, 'tp'), P('tp', None))
    out_specs = (P('dp', None), cache_spec, cache_spec, new_spec, new_spec)
    return jax.shard_map(local_step, mesh=mesh, in_specs=in_specs, out_specs=out_specs, check_vma=False)
```

time: 110 us -> 101 us (0.918)
  Pallas kernels: 107 us -> 96.8 us
  starting transfers between devices: 0 us -> 1.53 us
    pallas_call x2 -> x3, Pallas kernels: 107 us -> 96.8 us  [the longest x1 42.3 us: run_tail(): pl.pallas_call(tail_kernel, name='tail', out_shape=pltpu.VMEM((8, 16, DIM...]
    ppermute x0 -> x1, starting transfers between devices: none -> 1.53 us  [local_step(): oth = lax.ppermute(oth, 'tp', [(0, 1), (1, 0)])]
    unnamed x1 -> x3, local copies, waits for them, and re-layouts: 2.29 us -> 1.67 us
  transfers between devices with their start and end apart: 0 -> 1, of which waited for: 0 -> 0; matrix products, arithmetic and copies ran while one was open for 0% -> 0% of each run, Pallas kernels for 0% -> 24%
where the time goes in v3:
time: 101 us
  Pallas kernels  96.8 us (96%)
  local copies, waits for them, and re-layouts  1.67 us (2%)
  starting transfers between devices  1.53 us (2%)
    pallas_call x1, Pallas kernels, run_tail(): pl.pallas_call(tail_kernel, name='tail', out_shape=pltpu.VMEM((8, 16, DIM...  42.3 us
    pallas_call x1, Pallas kernels, run_front(): pl.pallas_call(front_kernel, name='front', out_shape=[new, new, dup, dup,...  30.7 us
    pallas_call x1, Pallas kernels, run_write(): pl.pallas_call(write_kernel, name='write', out_shape=[cache, cache, new,...  23.9 us
  transfers between devices with their start and end apart: 1, of which 0 were waited for; matrix products, arithmetic and copies ran while one was open for 0% of the time, Pallas kernels for 24%

profile of v3, /device:TPU:0, one launch (start us, length us, event | category | flops | bytes accessed | tf_op | source)
XLA Modules:
  0.0 100.7 jit_solution(5604069940725046474)
XLA Ops:
  0.6 30.7 %front.1 = (bf16[512,128]{1,0:T(8,128)(2,1)}, bf16[512,128]{1,0:T(8,128)(2,1)}, f32[1024,128]{1,0:T(8,128)}, f32[1024,128]{1,0:T(8,128)}, f32[16,4096]{1,0:T(8,128)}, /*index=5*/f32[16,4096]{1,0:T(8,128)}) custom-call(s32[128]{0:T(128)} %pos_s.3, bf16[128,4096]{1,0:T(8,128)(2,1)} %x_ref.1, s32[1,128]{1,0:T(1,128)} %bitcast.19, ...), custom_call_target="tpu_custom_call" | custom-call | flops 4000000000 | bytes 63000000 | tf_op jit(solution)/shard_map/front/pallas_call | solution.py:316
  31.3 1.5 %collective-permute-start = (f32[16,4096]{1,0:T(8,128)}, f32[16,4096]{1,0:T(8,128)S(1)}, u32[]{:S(2)}, u32[]{:S(2)}) collective-permute-start(f32[16,4096]{1,0:T(8,128)} %get-tuple-element.17), channel_id=1, source_target_pairs={{0,4},{4,0},{1,5},{5,1},{2,6},{6,2},{3,7},{7,3}} | collective-permute-start | bytes 786440 | tf_op jit(solution)/shard_map/ppermute | solution.py:658
  32.9 23.9 %write.1 = (bf16[128,512,128]{2,1,0:T(8,128)(2,1)}, bf16[128,512,128]{2,1,0:T(8,128)(2,1)}, bf16[512,128]{1,0:T(8,128)(2,1)}, bf16[512,128]{1,0:T(8,128)(2,1)}, f32[8,128]{1,0:T(8,128)}) custom-call(s32[128]{0:T(128)} %pos_s.3, f32[1024,128]{1,0:T(8,128)} %get-tuple-element.18.kdup, f32[1024,128]{1,0:T(8,128)} %get-tuple-element.19.vdup, ...), custom_call_target="tpu_custom_call" | custom-call | flops 5000000000 | bytes 67000000 | tf_op jit(solution)/shard_map/write/pallas_call | solution.py:410
  56.7 0.0 collective-permute-done.oth_in
  56.8 0.0 copy-start
  56.8 0.7 copy-done
  57.5 42.3 %tail.1 = bf16[8,16,4096]{2,1,0:T(8,128)(2,1)S(1)} custom-call(f32[16,4096]{1,0:T(8,128)} %get-tuple-element.16.own_in, f32[16,4096]{1,0:T(8,128)} %copy-done, bf16[8,16,4096]{2,1,0:T(8,128)(2,1)} %bitcast.16, bf16[32,128]{1,0:T(8,128)(2,1)} %bitcast.18, bf16[4096,7168]{1,0:T(8,128)(2,1)} %wg.1, bf16[4096,7168]{1,0:T(8,128)(2,1)} %wu.1, ...), custom_call_target="tpu_custom_call" | custom-call | flops 6000000000 | bytes 62000000 | tf_op jit(solution)/shard_map/tail/pallas_call | solution.py:622
  99.7 1.0 copy.20
Async XLA Ops:
  31.3 25.4 %collective-permute-start = (f32[16,4096]{1,0:T(8,128)}, f32[16,4096]{1,0:T(8,128)S(1)}, u32[]{:S(2)}, u32[]{:S(2)}) collective-permute-start(f32[16,4096]{1,0:T(8,128)} %get-tuple-element.17), channel_id=1, source_target_pairs={{0,4},{4,0},{1,5},{5,1},{2,6},{6,2},{3,7},{7,3}} | collective-permute-start | bytes 786440 | tf_op jit(solution)/shard_map/ppermute | solution.py:658
  56.8 0.7 copy-start

commit v4 on v3

--- a/solution.py
+++ b/solution.py
@@ -13,6 +13,7 @@
 F32 = jnp.float32
 BF16 = jnp.bfloat16
 MIB = 2**20
+VMEM_MAX = 67043328
 
 ROWS = 128
 DIM = 4096
@@ -26,7 +27,7 @@
 PAIR = 2
 M_AT = pl.ds(256, PAIR)
 L_AT = pl.ds(258, PAIR)
-RING = 4
+RING = 6
 
 def rms(x, gain_ref):
     ms = jnp.mean(jnp.square(x), axis=-1, keepdims=True)
@@ -127,8 +128,9 @@
         for c in wcp[j]:
             c.wait()
         y = jnp.dot(n_s[...], wbuf[j], preferred_element_type=F32)
-        for c in cache_copies(1 + j):
-            c.start()
+        for t in range(1 + j, RING if j == 2 else 2 + j):
+            for c in cache_copies(t):
+                c.start()
         for hh in range(4):
             yh = y[:, hh * HD : (hh + 1) * HD]
             if j == 0 and hh < 2:
@@ -201,37 +203,35 @@
     }
     send_a = rc(o_s.at[pl.ds(pair["a"], 2)], rba, bsem.at[0], dev_c)
     send_b = rc(o_s.at[pl.ds(pair["b"], 2)], rbb, bsem.at[1], dev_c)
-    send_x = rc(ob.at[pl.ds(0, 2)], rbx, bsem.at[2], dev_x)
+    send_x = [rc(ob.at[q], rbx.at[q], bsem.at[2 + q], dev_x) for q in range(PAIR)]
+
+    def patched(dup, buf, t, b, row, lim):
+        hit = slotb[...] == lax.broadcast(lim.astype(F32), (SLOTS * KVH, HD)).astype(BF16)
+        d = dup[pl.ds(pl.multiple_of(row * 8, 8), 8), :]
+        d = jnp.concatenate([d, d], axis=0).astype(BF16)
+        d = jnp.concatenate([d] * 32, axis=0)
+        return jnp.where(hit, d, buf[t % RING, b])
 
     def block(t, _):
         r = row_block(t)
         for c in cache_copies(t):
             c.wait()
 
-        @pl.when(t == 4)
+        @pl.when(t == 2)
         def _():
             for c in ocp:
                 c.start()
 
         for half in range(PAIR):
-            sc, lims, vals = [], [], []
+            sc, lims = [], []
             for b in range(8):
                 row = r * 16 + half * 8 + b
                 lim = pos_s[row] - sp * SLOTS
                 lims.append(lim)
-                hit = slotb[...] == lax.broadcast(lim.astype(F32), (SLOTS * KVH, HD)).astype(BF16)
-                new = pl.ds(pl.multiple_of(row * 8, 8), 8)
-                kv = []
-                for dup, ref in ((kdup, kbuf), (vdup, vbuf)):
-                    d = dup[new, :]
-                    d = jnp.concatenate([d, d], axis=0).astype(BF16)
-                    d = jnp.concatenate([d] * 32, axis=0)
-                    kv.append(jnp.where(hit, d, ref[t % RING, half * 8 + b]))
-                vals.append(kv[1])
                 q = qf[pl.ds(pl.multiple_of(row * QH, QH), QH), :].astype(BF16)
                 sc.append(
                     lax.dot_general(
-                        q, kv[0], (((1,), (1,)), ((), ())), preferred_element_type=F32
+                        q, patched(kdup, kbuf, t, half * 8 + b, row, lim), (((1,), (1,)), ((), ())), preferred_element_type=F32
                     )
                 )
             ms, ls = [], []
@@ -242,7 +242,8 @@
                 w = jnp.exp(s - m)
                 ms.append(m)
                 ls.append(jnp.sum(w, axis=-1, keepdims=True))
-                o = jnp.dot(w.astype(BF16), vals[b], preferred_element_type=F32)
+                v = patched(vdup, vbuf, t, half * 8 + b, r * 16 + half * 8 + b, lims[b])
+                o = jnp.dot(w.astype(BF16), v, preferred_element_type=F32)
                 o_s[r, pl.ds((half * 8 + b) * QH, QH), :] = o
             m = jnp.concatenate(ms, axis=0)
             l = jnp.concatenate(ls, axis=0)
@@ -253,12 +254,14 @@
         def _():
             send_a.start()
 
-        @pl.when(t == 3)
-        def _():
-            send_a.wait_recv()
-            for q in range(PAIR):
+        for q in range(PAIR):
+
+            @pl.when(t == 2 + q)
+            def _():
+                if q == 0:
+                    send_a.wait_recv()
                 merge_into(ob.at[q], o_s.at[pair["x"] + q], rba.at[q])
-            send_x.start()
+                send_x[q].start()
 
         @pl.when(t == 5)
         def _():
@@ -275,8 +278,8 @@
     send_b.wait_recv()
     for q in range(PAIR):
         merge_into(ob.at[2 + q], o_s.at[pair["own"] + q], rbb.at[q])
-    send_x.wait_recv()
     for q in range(PAIR):
+        send_x[q].wait_recv()
 
         def put(g, v):
             ofin[pl.ds(q * 256 + g * 128, 128), :] = v
@@ -298,7 +301,7 @@
         cs = pl.ds(i * 1024, 1024)
         own_out[:, cs] = jnp.where(yi == 0, v[:16], v[16:])
         oth_out[:, cs] = jnp.where(yi == 0, v[16:], v[:16])
-    for c in qcp + [send_a, send_b, send_x]:
+    for c in qcp + send_x + [send_a, send_b]:
         c.wait_send()
 
 
@@ -338,10 +341,10 @@
             pltpu.SemaphoreType.DMA((12,)),
             pltpu.SemaphoreType.DMA((2, RING)),
             pltpu.SemaphoreType.DMA((4, 2)),
-            pltpu.SemaphoreType.DMA((3, 2)),
+            pltpu.SemaphoreType.DMA((4, 2)),
         ],
         compiler_params=pltpu.CompilerParams(
-            collective_id=1, has_side_effects=True, vmem_limit_bytes=56 * MIB
+            collective_id=1, has_side_effects=True, vmem_limit_bytes=60 * MIB
         ),
         cost_estimate=pl.CostEstimate(flops=4 * 10**9, bytes_accessed=63 * 10**6, transcendentals=10**6),
     )(
@@ -350,7 +353,11 @@
     )
 
 
-def write_kernel(pos_s, kdup, vdup, kn, vn, k_in, v_in, k_out, v_out, kn_out, vn_out, tok, kbuf, vbuf, isem, osem):
+def write_kernel(
+    pos_s, kdup_in, vdup_in, kn_in, vn_in, k_in, v_in,
+    k_out, v_out, kn_out, vn_out, tok,
+    kbuf, vbuf, kdup, vdup, kn, vn, isem, osem, ssem, nsem,
+):
     sp = lax.axis_index("sp")
 
     def copies_in(i, s):
@@ -367,12 +374,23 @@
             pltpu.make_async_copy(vbuf.at[s], v_out.at[rows], osem.at[1, s]),
         )
 
+    small = [
+        pltpu.make_async_copy(a, b, ssem.at[i])
+        for i, (a, b) in enumerate(((kdup_in, kdup), (vdup_in, vdup), (kn_in, kn), (vn_in, vn)))
+    ]
+    new = [
+        pltpu.make_async_copy(a, b, nsem.at[i]) for i, (a, b) in enumerate(((kn, kn_out), (vn, vn_out)))
+    ]
+    for c in small:
+        c.start()
     for i in range(WSTEPS):
         for c in copies_in(i, i):
             c.start()
-    kn_out[...] = kn[...]
-    vn_out[...] = vn[...]
     tok[...] = jnp.zeros_like(tok)
+    for c in small:
+        c.wait()
+    for c in new:
+        c.start()
     r16 = lax.broadcasted_iota(jnp.int32, (16, HD), 0) >> 2
 
     def block(r, _):
@@ -385,9 +403,9 @@
             cl = jnp.clip(lim, 0, SLOTS - 1)
             at = pl.ds(pl.multiple_of((cl >> 2) * 16, 16), 16)
             hit = r16 == jnp.where(lim == cl, cl & 3, -1)
-            new = pl.ds(pl.multiple_of(row * 8, 8), 8)
+            of_row = pl.ds(pl.multiple_of(row * 8, 8), 8)
             for dup, buf in ((kdup, kbuf), (vdup, vbuf)):
-                d = dup[new, :]
+                d = dup[of_row, :]
                 d = jnp.concatenate([d, d], axis=0).astype(BF16)
                 buf[s, b, at, :] = jnp.where(hit, d, buf[s, b, at, :])
         return 0
@@ -399,6 +417,8 @@
     for i in range(WSTEPS):
         for c in copies_out(i, i):
             c.wait()
+    for c in new:
+        c.wait()
 
 
 def run_write(pos, kdup, vdup, kn, vn, k_blk, v_blk):
@@ -406,20 +426,28 @@
     hbm = pl.BlockSpec(memory_space=pl.ANY)
     cache = jax.ShapeDtypeStruct((ROWS, SLOTS * KVH, HD), BF16)
     new = jax.ShapeDtypeStruct((ROWS * KVH, HD), BF16)
+    dup = pltpu.VMEM((ROWS * 8, HD), F32)
+    small = pltpu.VMEM((ROWS * KVH, HD), BF16)
     ring = pltpu.VMEM((WSTEPS, WROWS, SLOTS * KVH, HD), BF16)
     return pl.pallas_call(
         write_kernel,
         name="write",
         out_shape=[cache, cache, new, new, jax.ShapeDtypeStruct((8, 128), F32)],
-        in_specs=[pl.BlockSpec(memory_space=pltpu.SMEM), vm, vm, vm, vm, hbm, hbm],
-        out_specs=[hbm, hbm, vm, vm, vm],
+        in_specs=[pl.BlockSpec(memory_space=pltpu.SMEM)] + [hbm] * 6,
+        out_specs=[hbm] * 4 + [vm],
         scratch_shapes=[
             ring,
             ring,
+            dup,
+            dup,
+            small,
+            small,
             pltpu.SemaphoreType.DMA((2, WSTEPS)),
             pltpu.SemaphoreType.DMA((2, WSTEPS)),
+            pltpu.SemaphoreType.DMA((4,)),
+            pltpu.SemaphoreType.DMA((2,)),
         ],
-        compiler_params=pltpu.CompilerParams(vmem_limit_bytes=56 * MIB),
+        compiler_params=pltpu.CompilerParams(vmem_limit_bytes=VMEM_MAX),
         cost_estimate=pl.CostEstimate(flops=5 * 10**9, bytes_accessed=67 * 10**6, transcendentals=0),
     )(
         pos, kdup, vdup, kn, vn,

time: 101 us -> 98.1 us (0.971)
  Pallas kernels: 96.8 us -> 94.8 us
    pallas_call x1, Pallas kernels: 30.7 us -> 29.1 us  [run_front(): pl.pallas_call(front_kernel, name='front', out_shape=[new, new, dup, dup,...]
where the time goes in v4:
time: 98.1 us; the launch traced here: 98 us
  Pallas kernels  94.8 us (97%)
  starting transfers between devices  1.54 us (2%)
    pallas_call x1, Pallas kernels, run_tail(): pl.pallas_call(tail_kernel, name='tail', out_shape=pltpu.VMEM((8, 16, DIM...  42.2 us
    pallas_call x1, Pallas kernels, run_front(): pl.pallas_call(front_kernel, name='front', out_shape=[new, new, dup, dup,...  29.1 us
    pallas_call x1, Pallas kernels, run_write(): pl.pallas_call(write_kernel, name='write', out_shape=[cache, cache, new,...  23.6 us
  transfers between devices with their start and end apart: 1, of which 0 were waited for; matrix products, arithmetic and copies ran while one was open for 0% of the time, Pallas kernels for 24%

profile of v4, /device:TPU:0, one launch (start us, length us, event | category | flops | bytes accessed | tf_op | source)
XLA Modules:
  0.0 98.0 jit_solution(8653884004887162851)
XLA Ops:
  0.6 29.1 %front.1 = (bf16[512,128]{1,0:T(8,128)(2,1)}, bf16[512,128]{1,0:T(8,128)(2,1)}, f32[1024,128]{1,0:T(8,128)}, f32[1024,128]{1,0:T(8,128)}, f32[16,4096]{1,0:T(8,128)}, /*index=5*/f32[16,4096]{1,0:T(8,128)}) custom-call(s32[128]{0:T(128)} %pos_s.3, bf16[128,4096]{1,0:T(8,128)(2,1)} %x_ref.1, s32[1,128]{1,0:T(1,128)} %bitcast.19, ...), custom_call_target="tpu_custom_call" | custom-call | flops 4000000000 | bytes 63000000 | tf_op jit(solution)/shard_map/front/pallas_call | solution.py:319
  29.7 1.5 %collective-permute-start = (f32[16,4096]{1,0:T(8,128)}, f32[16,4096]{1,0:T(8,128)}, u32[]{:S(2)}, u32[]{:S(2)}) collective-permute-start(f32[16,4096]{1,0:T(8,128)} %get-tuple-element.17), channel_id=1, source_target_pairs={{0,4},{4,0},{1,5},{5,1},{2,6},{6,2},{3,7},{7,3}} | collective-permute-start | bytes 786440 | tf_op jit(solution)/shard_map/ppermute | solution.py:686
  31.2 23.6 %write.1 = (bf16[128,512,128]{2,1,0:T(8,128)(2,1)}, bf16[128,512,128]{2,1,0:T(8,128)(2,1)}, bf16[512,128]{1,0:T(8,128)(2,1)}, bf16[512,128]{1,0:T(8,128)(2,1)}, f32[8,128]{1,0:T(8,128)}) custom-call(s32[128]{0:T(128)} %pos_s.3, f32[1024,128]{1,0:T(8,128)} %get-tuple-element.18.kdup_in, f32[1024,128]{1,0:T(8,128)} %get-tuple-element.19.vdup_in, ...), custom_call_target="tpu_custom_call" | custom-call | flops 5000000000 | bytes 67000000 | tf_op jit(solution)/shard_map/write/pallas_call | solution.py:432
  54.8 0.0 collective-permute-done.oth_in
  54.8 42.2 %tail.1 = bf16[8,16,4096]{2,1,0:T(8,128)(2,1)S(1)} custom-call(f32[16,4096]{1,0:T(8,128)} %get-tuple-element.16.own_in, f32[16,4096]{1,0:T(8,128)} %collective-permute-done.oth_in, bf16[8,16,4096]{2,1,0:T(8,128)(2,1)} %bitcast.16, bf16[32,128]{1,0:T(8,128)(2,1)} %bitcast.18, bf16[4096,7168]{1,0:T(8,128)(2,1)} %wg.1, bf16[4096,7168]{1,0:T(8,128)(2,1)} %wu.1, ...), custom_call_target="tpu_custom_call" | custom-call | flops 6000000000 | bytes 62000000 | tf_op jit(solution)/shard_map/tail/pallas_call | solution.py:650
  97.0 1.0 copy.20
Async XLA Ops:
  29.7 25.1 %collective-permute-start = (f32[16,4096]{1,0:T(8,128)}, f32[16,4096]{1,0:T(8,128)}, u32[]{:S(2)}, u32[]{:S(2)}) collective-permute-start(f32[16,4096]{1,0:T(8,128)} %get-tuple-element.17), channel_id=1, source_target_pairs={{0,4},{4,0},{1,5},{5,1},{2,6},{6,2},{3,7},{7,3}} | collective-permute-start | bytes 786440 | tf_op jit(solution)/shard_map/ppermute | solution.py:686

commit v5 on v4

--- a/solution.py
+++ b/solution.py
@@ -153,7 +153,7 @@
                 qcp[2].start()
             else:
                 qcp[3].start()
-    for c in qcp:
+    for c in qcp[:PAIR]:
         c.wait_recv()
     for i, (dup, out) in enumerate(((kdup, kn_out), (vdup, vn_out))):
         for h in range(KVH):
@@ -162,8 +162,11 @@
             for rep in range(PAIR):
                 dup[pl.ds(rep * KVH + h, ROWS, stride=8), :] = v
         out[...] = ofin[...].astype(BF16)
-    for h in range(QH):
-        qf[pl.ds(h, ROWS, stride=QH), :] = qraw[h]
+    for j, c in enumerate(qcp[PAIR:]):
+        c.wait_recv()
+        for h in range(QH):
+            if h // KVH % PAIR == j:
+                qf[pl.ds(h, ROWS, stride=QH), :] = qraw[h]
 
     col = lax.broadcasted_iota(jnp.int32, (QH, SLOTS * KVH), 1)
     hrow = lax.broadcasted_iota(jnp.int32, (QH, SLOTS * KVH), 0)

time: 98.1 us -> 97.6 us (level)
  no operation moved by 1% of the time
where the time goes in v5:
time: 97.6 us; the launch traced here: 97.4 us
  Pallas kernels  94.2 us (97%)
  starting transfers between devices  1.54 us (2%)
    pallas_call x1, Pallas kernels, run_tail(): pl.pallas_call(tail_kernel, name='tail', out_shape=pltpu.VMEM((8, 16, DIM...  42.1 us
    pallas_call x1, Pallas kernels, run_front(): pl.pallas_call(front_kernel, name='front', out_shape=[new, new, dup, dup,...  28.5 us
    pallas_call x1, Pallas kernels, run_write(): pl.pallas_call(write_kernel, name='write', out_shape=[cache, cache, new,...  23.6 us
  transfers between devices with their start and end apart: 1, of which 0 were waited for; matrix products, arithmetic and copies ran while one was open for 0% of the time, Pallas kernels for 24%

profile of v5, /device:TPU:0, one launch (start us, length us, event | category | flops | bytes accessed | tf_op | source)
XLA Modules:
  0.0 97.4 jit_solution(2504394087604465151)
XLA Ops:
  0.6 28.5 %front.1 = (bf16[512,128]{1,0:T(8,128)(2,1)}, bf16[512,128]{1,0:T(8,128)(2,1)}, f32[1024,128]{1,0:T(8,128)}, f32[1024,128]{1,0:T(8,128)}, f32[16,4096]{1,0:T(8,128)}, /*index=5*/f32[16,4096]{1,0:T(8,128)}) custom-call(s32[128]{0:T(128)} %pos_s.3, bf16[128,4096]{1,0:T(8,128)(2,1)} %x_ref.1, s32[1,128]{1,0:T(1,128)} %bitcast.19, ...), custom_call_target="tpu_custom_call" | custom-call | flops 4000000000 | bytes 63000000 | tf_op jit(solution)/shard_map/front/pallas_call | solution.py:322
  29.2 1.5 %collective-permute-start = (f32[16,4096]{1,0:T(8,128)}, f32[16,4096]{1,0:T(8,128)}, u32[]{:S(2)}, u32[]{:S(2)}) collective-permute-start(f32[16,4096]{1,0:T(8,128)} %get-tuple-element.17), channel_id=1, source_target_pairs={{0,4},{4,0},{1,5},{5,1},{2,6},{6,2},{3,7},{7,3}} | collective-permute-start | bytes 786440 | tf_op jit(solution)/shard_map/ppermute | solution.py:689
  30.7 23.6 %write.1 = (bf16[128,512,128]{2,1,0:T(8,128)(2,1)}, bf16[128,512,128]{2,1,0:T(8,128)(2,1)}, bf16[512,128]{1,0:T(8,128)(2,1)}, bf16[512,128]{1,0:T(8,128)(2,1)}, f32[8,128]{1,0:T(8,128)}) custom-call(s32[128]{0:T(128)} %pos_s.3, f32[1024,128]{1,0:T(8,128)} %get-tuple-element.18.kdup_in, f32[1024,128]{1,0:T(8,128)} %get-tuple-element.19.vdup_in, ...), custom_call_target="tpu_custom_call" | custom-call | flops 5000000000 | bytes 67000000 | tf_op jit(solution)/shard_map/write/pallas_call | solution.py:435
  54.3 0.0 collective-permute-done.oth_in
  54.3 42.1 %tail.1 = bf16[8,16,4096]{2,1,0:T(8,128)(2,1)S(1)} custom-call(f32[16,4096]{1,0:T(8,128)} %get-tuple-element.16.own_in, f32[16,4096]{1,0:T(8,128)} %collective-permute-done.oth_in, bf16[8,16,4096]{2,1,0:T(8,128)(2,1)} %bitcast.16, bf16[32,128]{1,0:T(8,128)(2,1)} %bitcast.18, bf16[4096,7168]{1,0:T(8,128)(2,1)} %wg.1, bf16[4096,7168]{1,0:T(8,128)(2,1)} %wu.1, ...), custom_call_target="tpu_custom_call" | custom-call | flops 6000000000 | bytes 62000000 | tf_op jit(solution)/shard_map/tail/pallas_call | solution.py:653
  96.5 1.0 copy.20
Async XLA Ops:
  29.2 25.1 %collective-permute-start = (f32[16,4096]{1,0:T(8,128)}, f32[16,4096]{1,0:T(8,128)}, u32[]{:S(2)}, u32[]{:S(2)}) collective-permute-start(f32[16,4096]{1,0:T(8,128)} %get-tuple-element.17), channel_id=1, source_target_pairs={{0,4},{4,0},{1,5},{5,1},{2,6},{6,2},{3,7},{7,3}} | collective-permute-start | bytes 786440 | tf_op jit(solution)/shard_map/ppermute | solution.py:689
